TPU v7x, 128 devices: a whole 4x4x4 slice. The times are simulated.
128 devices in a mesh: grp: 16 (over z, y), blk: 8 (over x, core).
Axes of the slice: x: 4, y: 4, z: 4, core: 2. Of those that a mesh axis runs over, the one named last changes fastest.
Arguments:
- queries: bfloat16 [81920, 2048], P(('grp', 'blk')), may hold values from -6 to 6
- key_rows: bfloat16 [81920, 256], P(('grp', 'blk')), may hold values from -6 to 6
- value_rows: bfloat16 [81920, 256], P(('grp', 'blk')), may hold values from -6 to 6
- out_grad: bfloat16 [81920, 2048], P(('grp', 'blk')), may hold values from -12 to 12
- attn_out: bfloat16 [81920, 2048], P(('grp', 'blk')), may hold values from -6 to 6
- log_norm: float32 [81920, 16], P(('grp', 'blk')), may hold values from 4 to 7
- held_block: int32 [128], replicated, may hold values from 0 to 127, as said below
- key_block: int32 [128], replicated, may hold values from 0 to 127, as said below
Outputs:
- query_grad: bfloat16 [81920, 2048], P(('grp', 'blk'))
- key_grad: bfloat16 [81920, 256], P(('grp', 'blk'))
- value_grad: bfloat16 [81920, 256], P(('grp', 'blk'))
Inputs may be any that keep to these rules, and one draw needn't show every extreme that they name: held_block is a permutation of the 128 blocks. key_block[d] <= held_block[d] for every d; a key block may be paired with many query blocks or none.
All inputs are finite; a program needn't handle non-finite values.
Results may differ from a plain program's by a relative error of at most 0.0069.
Values may be sent and summed in bfloat16 or wider, within the bound.
No kernel may reach another device: no remote copies, remote signals or barrier semaphores. Data moves between devices by JAX's collectives and lax.ppermute only.
A program may use at most 192 MiB of HBM per device.

v0:
```python
import jax
import jax.numpy as jnp
from jax import lax
from jax.sharding import PartitionSpec as P

H = 16
KVH = 2
DH = 128


def pair_grads(query, dout, outs, norms, kv_rows, diag):
    rows = query.shape[0]
    group = H // KVH
    scale = DH ** (-0.5)
    delta = jnp.sum(
        (dout.astype(jnp.float32) * outs.astype(jnp.float32)).reshape(rows, H, DH), axis=-1
    )
    row_ids = lax.broadcasted_iota(jnp.int32, (rows, rows), 0)
    col_ids = lax.broadcasted_iota(jnp.int32, (rows, rows), 1)
    keep = jnp.logical_or(jnp.logical_not(diag), col_ids <= row_ids)
    query_parts, key_parts, value_parts = ([], [], [])
    for head in range(KVH):
        width = group * DH
        q_head = query[:, head * width : (head + 1) * width].reshape(rows, group, DH)
        o_head = dout[:, head * width : (head + 1) * width].reshape(rows, group, DH)
        k_head = kv_rows[:, head * DH : (head + 1) * DH]
        v_head = kv_rows[:, (KVH + head) * DH : (KVH + head + 1) * DH]
        scores = (
            jnp.einsum("igd,jd->gij", q_head, k_head, preferred_element_type=jnp.float32) * scale
        )
        lse_head = jnp.transpose(norms[:, head * group : (head + 1) * group])[:, :, None]
        probs = jnp.where(keep[None], jnp.exp(scores - lse_head), 0.0)
        probs_low = probs.astype(jnp.bfloat16)
        dv_head = jnp.einsum("gij,igd->jd", probs_low, o_head, preferred_element_type=jnp.float32)
        dprob = jnp.einsum("igd,jd->gij", o_head, v_head, preferred_element_type=jnp.float32)
        delta_head = jnp.transpose(delta[:, head * group : (head + 1) * group])[:, :, None]
        dscore = (probs * (dprob - delta_head) * scale).astype(jnp.bfloat16)
        dq_head = jnp.einsum("gij,jd->igd", dscore, k_head, preferred_element_type=jnp.float32)
        dk_head = jnp.einsum("gij,igd->jd", dscore, q_head, preferred_element_type=jnp.float32)
        query_parts.append(dq_head.reshape(rows, width))
        key_parts.append(dk_head)
        value_parts.append(dv_head)
    query_grad = jnp.concatenate(query_parts, axis=1).astype(jnp.bfloat16)
    pair_term = jnp.concatenate(key_parts + value_parts, axis=1).astype(jnp.bfloat16)
    return (query_grad, pair_term)


def per_device(queries, key_rows, value_rows, out_grad, attn_out, log_norm, held_block, key_block):
    n_grp = lax.axis_size("grp")
    n_blk = lax.axis_size("blk")
    g_index = lax.axis_index("grp")
    b_index = lax.axis_index("blk")
    count = n_grp * n_blk
    own_index = g_index * n_blk + b_index
    positions = jnp.arange(count, dtype=jnp.int32)
    holder = jnp.sum(
        jnp.where(held_block[None, :] == key_block[:, None], positions[None, :], 0), axis=1
    )
    hold_grp = (holder // n_blk).reshape(n_grp, n_blk)
    hold_blk = (holder % n_blk).reshape(n_grp, n_blk)
    own_hold = lax.dynamic_index_in_dim(holder, own_index, 0, keepdims=False)
    own_blk = own_hold % n_blk
    own_query = lax.dynamic_index_in_dim(held_block, own_index, 0, keepdims=False)
    own_key = lax.dynamic_index_in_dim(key_block, own_index, 0, keepdims=False)
    diag = own_query == own_key
    kv_local = jnp.concatenate([key_rows, value_rows], axis=1)
    row_grp = lax.dynamic_index_in_dim(hold_grp, g_index, 0, keepdims=False)
    row_blk = lax.dynamic_index_in_dim(hold_blk, g_index, 0, keepdims=False)
    slots = jnp.arange(n_grp, dtype=jnp.int32)
    select = jnp.logical_and(
        (row_blk == b_index)[:, None], row_grp[:, None] == slots[None, :]
    ).astype(jnp.bfloat16)
    gathered = lax.all_gather(kv_local[None], "grp", axis=0, tiled=True)
    outgoing = jnp.einsum(
        "bg,grc->brc", select, gathered, preferred_element_type=jnp.float32
    ).astype(jnp.bfloat16)
    incoming = lax.all_to_all(outgoing, "blk", split_axis=0, concat_axis=0, tiled=True)
    kv_rows = lax.dynamic_index_in_dim(incoming, own_blk, 0, keepdims=False)
    query_grad, pair_term = pair_grads(queries, out_grad, attn_out, log_norm, kv_rows, diag)
    targets = jnp.arange(n_blk, dtype=jnp.int32)
    sending = jnp.where(
        (targets == own_blk)[:, None, None], pair_term[None], jnp.zeros_like(pair_term)[None]
    )
    returned = lax.all_to_all(sending, "blk", split_axis=0, concat_axis=0, tiled=True)
    pooled = jnp.einsum("bg,brc->grc", select, returned, preferred_element_type=jnp.float32)
    summed = lax.psum_scatter(
        pooled.astype(jnp.bfloat16), "grp", scatter_dimension=0, tiled=True
    ).astype(jnp.float32)[0]
    summed = summed.astype(jnp.bfloat16)
    return (query_grad, summed[:, : KVH * DH], summed[:, KVH * DH :])


def solution(mesh):
    return jax.shard_map(
        per_device,
        mesh=mesh,
        in_specs=(
            P(("grp", "blk"), None),
            P(("grp", "blk"), None),
            P(("grp", "blk"), None),
            P(("grp", "blk"), None),
            P(("grp", "blk"), None),
            P(("grp", "blk"), None),
            P(),
            P(),
        ),
        out_specs=(P(("grp", "blk"), None), P(("grp", "blk"), None), P(("grp", "blk"), None)),
        check_vma=False,
    )
```

profile of v0, /device:TPU:1, one launch (start us, length us, event | category | flops | bytes accessed | tf_op | source)
XLA Modules:
  0.0 385.3 jit_solution(9617832846220431775)
XLA Ops:
  7.2 2.0 pad_maximum_fusion.1
  9.2 0.8 select_reduce_fusion
  10.0 0.1 reduce_sum.21
  10.2 84.0 %all-gather.3.cloned.1.call-done = bf16[10240,512]{1,0:T(8,128)(2,1)} async-done(((bf16[640,512]{1,0:T(8,128)(2,1)}), bf16[10240,512]{1,0:T(8,128)(2,1)}) %all-gather.3.cloned.1.call-update) | async-done | bytes 10485776 | tf_op jit(solution)/shard_map/all_gather | solution.py:73
  94.2 10.0 %fusion.21 = bf16[8,640,512]{2,0,1:T(8,128)(2,1)S(1)} fusion(bf16[16,640,512]{2,1,0:T(8,128)(2,1)} %bitcast.127, s32[8]{0:T(128)S(1)} %fusion.51, pred[8]{0:T(512)(128)(4,1)S(1)} %compare_bitcast_fusion), kind=kOutput, calls=%fused_computation.26 | convolution fusion | flops 86507776 | bytes 15728680 | tf_op jit(solution)/shard_map/bg,grc->brc/dot_general | solution.py:74
  104.1 4.2 %copy.58 = bf16[8,640,512]{2,1,0:T(8,128)(2,1)} copy(bf16[8,640,512]{2,0,1:T(8,128)(2,1)S(1)} %fusion.21) | data formatting | bytes 10485760 | tf_op jit(solution)/shard_map/convert_element_type | solution.py:76
  108.4 5.5 %all-to-all-start = ((bf16[8,640,512]{2,1,0:T(8,128)(2,1)}), bf16[8,640,512]{2,1,0:T(8,128)(2,1)}, u32[]{:S(2)}, u32[]{:S(2)}) async-start(bf16[8,640,512]{2,1,0:T(8,128)(2,1)} %copy.58), calls=%async_computation | async-start | bytes 10485760 | tf_op jit(solution)/shard_map/all_to_all | solution.py:77
  113.9 0.6 dynamic_slice.26
  114.5 0.6 dynamic_slice.25
  115.0 0.6 dynamic_slice.23
  118.9 3.6 fusion.57
  122.5 2.6 copy.96
  125.1 2.4 copy.98
  127.5 1.8 fusion.56
  129.3 2.5 copy.97
  131.8 2.4 copy.99
  134.2 2.7 multiply_bitcast_fusion
  136.9 3.5 copy.100
  140.5 4.0 %reduce_sum.22 = f32[640,16]{1,0:T(8,128)S(1)} reduce(f32[640,16,128]{2,1,0:T(8,128)} %bitcast.126, f32[]{:T(128)} %constant.68.clone.1), dimensions={2}, to_apply=%region_1.2 | reduce | flops 1300480 | bytes 5283844 | tf_op jit(solution)/shard_map/reduce_sum | solution.py:15
  144.5 0.2 slice_bitcast_fusion.1
  144.7 0.1 copy.63
  144.8 0.1 copy.70
  144.9 0.9 fusion.24
  145.9 28.0 %all-to-all-done = bf16[8,640,512]{2,1,0:T(8,128)(2,1)} async-done(((bf16[8,640,512]{2,1,0:T(8,128)(2,1)}), bf16[8,640,512]{2,1,0:T(8,128)(2,1)}, u32[]{:S(2)}, u32[]{:S(2)}) %all-to-all-start) | async-done | bytes 5242912 | tf_op jit(solution)/shard_map/all_to_all | solution.py:77
  173.9 1.1 dynamic-slice_bitcast_fusion
  175.1 1.9 fusion.40
  176.9 2.7 fusion.33
  179.7 5.2 %fusion.2 = bf16[8,640,640]{1,2,0:T(8,128)(2,1)S(1)} fusion(f32[640,640,8]{1,0,2:T(8,128)S(1)} %fusion.40, bf16[640,8,128]{0,2,1:T(8,128)(2,1)S(1)} %bitcast.137, f32[8,640]{1,0:T(8,128)S(1)} %copy.70, f32[8,640]{1,0:T(8,128)S(1)} %get-tuple-element.16, pred[640,640]{0,1:T(8,128)(4,1)S(1)} %copy-done.7, bf16[640,512]{1,0:T(8,128)(2,1)S(1)} %dynamic-slice_bitcast_fusion), kind=kOutput, calls=%fused_computation.3 | convolution fusion | flops 861798400 | bytes 21585920 | tf_op jit(solution)/shard_map/igd,jd->gij/dot_general | solution.py:35
  184.9 2.1 fusion.32
  187.0 0.2 copy-done.3
  187.2 1.9 fusion.39
  189.1 2.7 fusion.36
  191.8 5.0 %fusion.7 = bf16[8,640,640]{1,2,0:T(8,128)(2,1)S(1)} fusion(f32[640,640,8]{1,0,2:T(8,128)S(1)} %fusion.39, bf16[640,8,128]{0,2,1:T(8,128)(2,1)S(1)} %bitcast.135, f32[8,640]{1,0:T(8,128)S(1)} %copy.63, f32[8,640]{1,0:T(8,128)S(1)} %get-tuple-element.15, pred[640,640]{0,1:T(8,128)(4,1)S(1)} %copy-done.7, bf16[640,512]{1,0:T(8,128)(2,1)S(1)} %dynamic-slice_bitcast_fusion), kind=kOutput, calls=%fused_computation.10 | convolution fusion | flops 861798400 | bytes 21585920 | tf_op jit(solution)/shard_map/igd,jd->gij/dot_general | solution.py:35
  196.8 2.7 copy-done.2
  199.4 2.1 fusion.31
  201.5 0.1 pad_maximum_fusion.2
  201.6 0.3 copy.79
  201.9 0.5 broadcast_select_fusion
  202.4 63.6 %all_to_all.10 = bf16[8,640,512]{2,1,0:T(8,128)(2,1)S(1)} all-to-all(bf16[8,640,512]{2,1,0:T(8,128)(2,1)S(1)} %broadcast_select_fusion), channel_id=1, replica_groups=mesh['grp'=16,'blk'=8] {'blk'}, dimensions={0} | all-to-all | bytes 10485760 | tf_op jit(solution)/shard_map/all_to_all | solution.py:84
  266.0 8.5 %convolution_convert_fusion = bf16[16,640,512]{2,0,1:T(8,128)(2,1)} fusion(bf16[8,640,512]{2,1,0:T(8,128)(2,1)S(1)} %all_to_all.10, s32[8]{0:T(128)S(1)} %fusion.51, pred[8]{0:T(512)(128)(4,1)S(1)} %compare_bitcast_fusion), kind=kOutput, calls=%fused_computation.18 | convolution fusion | flops 89129216 | bytes 15728680 | tf_op jit(solution)/shard_map/bg,brc->grc/dot_general | solution.py:85
  274.4 13.9 %copy.81 = bf16[16,640,512]{2,1,0:T(8,128)(2,1)} copy(bf16[16,640,512]{2,0,1:T(8,128)(2,1)} %convolution_convert_fusion) | data formatting | bytes 20971520 | tf_op jit(solution)/shard_map/convert_element_type | solution.py:87
  288.4 4.1 %convolution_convert_fusion.1 = bf16[128,8,640]{2,0,1:T(8,128)(2,1)S(1)} fusion(bf16[8,640,640]{1,2,0:T(8,128)(2,1)} %copy-done.1, bf16[640,512]{1,0:T(8,128)(2,1)S(1)} %dynamic-slice_bitcast_fusion), kind=kOutput, calls=%fused_computation.30 | convolution fusion | flops 839516160 | bytes 8028160 | tf_op jit(solution)/shard_map/gij,jd->igd/dot_general | solution.py:38
  292.4 0.7 copy.74
  293.1 5.1 %convolution_convert_fusion.2 = bf16[128,8,640]{2,0,1:T(8,128)(2,1)} fusion(bf16[8,640,640]{1,2,0:T(8,128)(2,1)} %copy-done.2, bf16[640,512]{1,0:T(8,128)(2,1)S(1)} %dynamic-slice_bitcast_fusion), kind=kOutput, calls=%fused_computation.31 | convolution fusion | flops 839516160 | bytes 8028160 | tf_op jit(solution)/shard_map/gij,jd->igd/dot_general | solution.py:38
  298.2 1.6 copy.73
  299.9 1.7 pad_maximum_fusion
  301.6 74.5 %reduce-scatter.4.cloned.1.call-done = bf16[1,640,512]{2,1,0:T(8,128)(2,1)} async-done(((bf16[16,640,512]{2,1,0:T(8,128)(2,1)}), bf16[1,640,512]{2,1,0:T(8,128)(2,1)}) %reduce-scatter.4.cloned.1.call-update) | async-done | bytes 655376
  376.1 1.9 fusion.58
  (29 shorter events, 0.2 us)
Async XLA Ops:
  7.2 87.0 %all-gather.3.cloned.1.call-start = ((), (), s32[]{:S(2)}) async-start(), calls=%async_computation.3 | async-start | bytes 11141120 | tf_op jit(solution)/shard_map/all_gather | solution.py:73
  108.4 5.5 %copy-start.9 = (s32[128]{0:T(128)S(1)}, s32[128]{0:T(128)}, u32[]{:S(2)}) copy-start(s32[128]{0:T(128)} %param.15) | copy-start | bytes 1540
  108.4 6.1 %copy-start.10 = (s32[128]{0:T(128)S(1)}, s32[128]{0:T(128)}, u32[]{:S(2)}) copy-start(s32[128]{0:T(128)} %param.14) | copy-start | bytes 1540
  108.4 65.5 %all-to-all-start = ((bf16[8,640,512]{2,1,0:T(8,128)(2,1)}), bf16[8,640,512]{2,1,0:T(8,128)(2,1)}, u32[]{:S(2)}, u32[]{:S(2)}) async-start(bf16[8,640,512]{2,1,0:T(8,128)(2,1)} %copy.58), calls=%async_computation | async-start | bytes 10485760 | tf_op jit(solution)/shard_map/all_to_all | solution.py:77
  113.9 262.2 %reduce-scatter.4.cloned.1.call-start = ((), (), s32[]{:S(2)}) async-start(), calls=%async_computation.4 | async-start | bytes 11141120
  118.9 8.6 %copy-start = (bf16[640,2048]{1,0:T(8,128)(2,1)S(1)}, bf16[640,2048]{1,0:T(8,128)(2,1)}, u32[]{:S(2)}) copy-start(bf16[640,2048]{1,0:T(8,128)(2,1)} %param.11) | copy-start | bytes 7864324
  140.5 5.4 %copy-start.8 = (f32[640,16]{0,1:T(8,128)S(1)}, f32[640,16]{0,1:T(8,128)}, u32[]{:S(2)}) copy-start(f32[640,16]{0,1:T(8,128)} %param.13) | copy-start | bytes 122884
  140.5 34.6 %copy-start.4 = (bf16[640,1024]{0,1:T(8,128)(2,1)S(1)}, bf16[640,1024]{0,1:T(8,128)(2,1)}, u32[]{:S(2)}) copy-start(bf16[640,1024]{0,1:T(8,128)(2,1)} %copy.98) | copy-start | bytes 3932164
  175.1 1.9 copy-start.6
  175.1 1.9 copy-start.7
  184.9 4.2 %copy-start.1 = (bf16[8,640,640]{1,2,0:T(8,128)(2,1)}, bf16[8,640,640]{1,2,0:T(8,128)(2,1)S(1)}, u32[]{:S(2)}) copy-start(bf16[8,640,640]{1,2,0:T(8,128)(2,1)S(1)} %fusion.2) | copy-start | bytes 19660804
  184.9 2.3 copy-start.3
  187.2 1.9 copy-start.5
  196.7 2.7 copy-start.2
Sparse Core Ops, SparseCore 0:
  10.7 83.4 all-gather.2
  288.5 87.5 reduce-scatter.3
where the time goes:
time: 393 us; the launch traced here: 385 us
  waiting for transfers between devices  187 us (48%)
  blocking collectives  63.6 us (16%)
  matrix products  51.1 us (13%)
  local copies, waits for them, and re-layouts  47.7 us (12%)
  between operations  18 us (5%)
  other arithmetic  12.8 us (3%)
  starting transfers between devices  5.54 us (1%)
    all_gather x1, waiting for transfers between devices, per_device(): gathered = lax.all_gather(kv_local[None], 'grp', axis=0, tiled=True)  84 us
    unnamed x3, waiting for transfers between devices  74.5 us
    all_to_all x1, blocking collectives, per_device(): lax.all_to_all(sending, 'blk', split_axis=0, concat_axis=0, tiled=True)  63.6 us
    all_to_all x1, waiting for transfers between devices, per_device(): lax.all_to_all(outgoing, 'blk', split_axis=0, concat_axis=0, tiled=True)  28 us
    unnamed x27, local copies, waits for them, and re-layouts  16.3 us
    convert_element_type x1, local copies, waits for them, and re-layouts, per_device(): pooled.astype(jnp.bfloat16)  13.9 us
    dot_general x2, matrix products, pair_grads(): jnp.einsum('igd,jd->gij', o_head, v_head, preferred_element_type=jnp.floa...  10.2 us
    dot_general x1, matrix products, per_device(): jnp.einsum('bg,grc->brc', select, gathered, preferred_element_type=jnp.fl...  9.96 us
  transfers between devices with their start and end apart: 3, of which 3 were waited for; matrix products, arithmetic and copies ran while one was open for 11% of the time, Pallas kernels for 0%

commit v1 on v0

v1 whole, which is shorter than its diff:
```python
import functools

import jax
import jax.numpy as jnp
from jax import lax
from jax.experimental import pallas as pl
from jax.experimental.pallas import tpu as pltpu
from jax.sharding import PartitionSpec as P

H = 16
KVH = 2
DH = 128
GROUP = H // KVH
AXES = ("grp", "blk")
SCALE = DH ** (-0.5)
LOG2E = 1.4426950408889634
STEP_HEADS = 2


def spread_kernel(k_ref, v_ref, out_ref):
    parts = out_ref.shape[0]
    depth = out_ref.shape[1]
    half = parts // 2
    for at, ref in enumerate((k_ref, v_ref)):
        turned = ref[...].T
        out_ref[at * half : (at + 1) * half] = turned.reshape(half, depth, turned.shape[1])


def fill_positions(held_ref, pos_ref):
    def put(e, carry):
        pos_ref[held_ref[e]] = e
        return carry

    lax.fori_loop(0, held_ref.shape[0], put, 0, unroll=8)


def select_kernel(held_ref, key_ref, in_ref, out_ref, pos_ref):
    fill_positions(held_ref, pos_ref)

    def move(d, carry):
        out_ref[d] = in_ref[pos_ref[key_ref[d]]]
        return carry

    lax.fori_loop(0, key_ref.shape[0], move, 0, unroll=8)


def pool_kernel(held_ref, key_ref, in_ref, out_ref, pos_ref, total_ref):
    fill_positions(held_ref, pos_ref)
    total_ref[...] = jnp.zeros_like(total_ref)

    def add(d, carry):
        at = pos_ref[key_ref[d]]
        total_ref[at] = total_ref[at] + in_ref[d].astype(jnp.float32)
        return carry

    lax.fori_loop(0, key_ref.shape[0], add, 0, unroll=8)
    out_ref[...] = total_ref[...].astype(out_ref.dtype)


def finish_kernel(in_ref, k_ref, v_ref):
    parts, depth, rows = in_ref.shape
    half = parts // 2
    for at, ref in enumerate((k_ref, v_ref)):
        flat = in_ref[at * half : (at + 1) * half].reshape(half * depth, rows)
        ref[...] = flat.T


def pair_kernel(
    off_ref, q_ref, do_ref, o_ref, norm_ref, kv_ref, dq_ref, term_ref,
    flat_ref, k_ref, dk_ref, dv_ref,
):
    step = pl.program_id(0)
    per_group = GROUP // STEP_HEADS
    c = step // per_group
    at = step % per_group
    rows = q_ref.shape[0]
    depth = kv_ref.shape[1]
    pieces = DH // depth

    @pl.when(step == 0)
    def _():
        flat_ref[...] = kv_ref[...].reshape(flat_ref.shape)

    @pl.when(at == 0)
    def _():
        k_ref[...] = flat_ref[pl.ds(pl.multiple_of(c * DH, DH), DH), :].T
        dk_ref[...] = jnp.zeros_like(dk_ref)
        dv_ref[...] = jnp.zeros_like(dv_ref)

    k_t = flat_ref[pl.ds(pl.multiple_of(c * DH, DH), DH), :]
    v_t = flat_ref[pl.ds(pl.multiple_of((KVH + c) * DH, DH), DH), :]
    k_rows = k_ref[...]
    limit = lax.broadcasted_iota(jnp.int32, (rows, 1), 0) + off_ref[0]
    keep = lax.broadcasted_iota(jnp.int32, (rows, rows), 1) <= limit
    norms = norm_ref[...]
    lanes = lax.broadcasted_iota(jnp.int32, norms.shape, 1)
    dk = dk_ref[...]
    dv = dv_ref[...]
    for sub in range(STEP_HEADS):
        cols = slice(sub * DH, (sub + 1) * DH)
        q = q_ref[:, cols]
        do = do_ref[:, cols]
        delta = jnp.sum(
            do.astype(jnp.float32) * o_ref[:, cols].astype(jnp.float32), axis=1, keepdims=True
        )
        lse = jnp.sum(
            jnp.where(lanes == step * STEP_HEADS + sub, norms, 0.0), axis=1, keepdims=True
        )
        s = jnp.dot(q, k_t, preferred_element_type=jnp.float32)
        dp = jnp.dot(do, v_t, preferred_element_type=jnp.float32)
        p = jnp.exp2(jnp.where(keep, s * (SCALE * LOG2E) - lse * LOG2E, -jnp.inf))
        ds = (p * (dp - delta)).astype(jnp.bfloat16)
        dq = jnp.dot(ds, k_rows, preferred_element_type=jnp.float32) * SCALE
        dq_ref[:, cols] = dq.astype(dq_ref.dtype)
        dv = dv + jnp.dot(do.T, p.astype(jnp.bfloat16), preferred_element_type=jnp.float32)
        dk = dk + jnp.dot(q.T, ds, preferred_element_type=jnp.float32)
    dk_ref[...] = dk
    dv_ref[...] = dv

    @pl.when(at == per_group - 1)
    def _():
        low_k = (dk_ref[...] * SCALE).astype(term_ref.dtype)
        low_v = dv_ref[...].astype(term_ref.dtype)
        term_ref[pl.ds(c * pieces, pieces)] = low_k.reshape(pieces, depth, rows)
        term_ref[pl.ds((KVH + c) * pieces, pieces)] = low_v.reshape(pieces, depth, rows)


def exchange(x):
    return lax.all_to_all(x, AXES, split_axis=0, concat_axis=0, tiled=True)


def per_device(queries, key_rows, value_rows, out_grad, attn_out, log_norm, held_block, key_block):
    count = lax.axis_size("grp") * lax.axis_size("blk")
    own = lax.axis_index("grp") * lax.axis_size("blk") + lax.axis_index("blk")
    rows = queries.shape[0]
    depth = 2 * KVH * DH // count
    piece = (count, depth, rows)
    low = jax.ShapeDtypeStruct(piece, jnp.bfloat16)
    vmem = pl.BlockSpec(memory_space=pltpu.VMEM)
    smem = pl.BlockSpec(memory_space=pltpu.SMEM)

    spread = pl.pallas_call(
        spread_kernel, out_shape=low, in_specs=[vmem] * 2, out_specs=vmem, name="spread"
    )(key_rows, value_rows)
    gathered = exchange(spread)
    chosen = pl.pallas_call(
        select_kernel,
        out_shape=low,
        in_specs=[smem, smem, vmem],
        out_specs=vmem,
        scratch_shapes=[pltpu.SMEM((count,), jnp.int32)],
        name="select",
    )(held_block, key_block, gathered)
    kv = exchange(chosen)

    own_query = lax.dynamic_index_in_dim(held_block, own, 0)
    own_key = lax.dynamic_index_in_dim(key_block, own, 0)
    off = jnp.where(own_query == own_key, 0, rows).astype(jnp.int32)
    width = STEP_HEADS * DH
    wide = pl.BlockSpec((rows, width), lambda s: (0, s))
    query_grad, term = pl.pallas_call(
        pair_kernel,
        grid=(H // STEP_HEADS,),
        out_shape=(jax.ShapeDtypeStruct(queries.shape, jnp.bfloat16), low),
        in_specs=[
            smem, wide, wide, wide,
            pl.BlockSpec(log_norm.shape, lambda s: (0, 0)),
            pl.BlockSpec(piece, lambda s: (0, 0, 0)),
        ],
        out_specs=(wide, pl.BlockSpec(piece, lambda s: (0, 0, 0))),
        scratch_shapes=[
            pltpu.VMEM((2 * KVH * DH, rows), jnp.bfloat16),
            pltpu.VMEM((rows, DH), jnp.bfloat16),
            pltpu.VMEM((DH, rows), jnp.float32),
            pltpu.VMEM((DH, rows), jnp.float32),
        ],
        compiler_params=pltpu.CompilerParams(
            dimension_semantics=("arbitrary",), vmem_limit_bytes=56 * 1024 * 1024
        ),
        name="pair",
    )(off, queries, out_grad, attn_out, log_norm, kv)

    returned = exchange(term)
    pooled = pl.pallas_call(
        pool_kernel,
        out_shape=low,
        in_specs=[smem, smem, vmem],
        out_specs=vmem,
        scratch_shapes=[pltpu.SMEM((count,), jnp.int32), pltpu.VMEM(piece, jnp.float32)],
        name="pool",
    )(held_block, key_block, returned)
    home = exchange(pooled)
    key_grad, value_grad = pl.pallas_call(
        finish_kernel,
        out_shape=(
            jax.ShapeDtypeStruct(key_rows.shape, jnp.bfloat16),
            jax.ShapeDtypeStruct(value_rows.shape, jnp.bfloat16),
        ),
        in_specs=[vmem],
        out_specs=(vmem, vmem),
        name="finish",
    )(home)
    return (query_grad, key_grad, value_grad)


def solution(mesh):
    rows = P(AXES, None)
    return jax.shard_map(
        per_device,
        mesh=mesh,
        in_specs=(rows,) * 6 + (P(), P()),
        out_specs=(rows, rows, rows),
        check_vma=False,
    )
```

time: 393 us -> 122 us (0.31); the launches traced: 385 us -> 122 us
  waiting for transfers between devices: 187 us -> 11.7 us
  matrix products: 51.1 us -> 0 us
  local copies, waits for them, and re-layouts: 47.7 us -> 2.91 us
  Pallas kernels: 0 us -> 33.2 us
  between operations: 18 us -> 1.9 us
  other arithmetic: 12.8 us -> 0 us
    all_gather x1 -> x0, waiting for transfers between devices: 84 us -> none  [per_device(): gathered = lax.all_gather(kv_local[None], 'grp', axis=0, tiled=True)]
    unnamed x3 -> x0, waiting for transfers between devices: 74.5 us -> none
    dot_general x12 -> x0, matrix products: 51.1 us -> none  [the longest x2 10.2 us: pair_grads(): jnp.einsum('igd,jd->gij', o_head, v_head, preferred_element_type=jnp.floa...]
    pallas_call x0 -> x5, Pallas kernels: none -> 33.2 us  [the longest x1 23.6 us: per_device(): pl.pallas_call(pair_kernel, grid=(H // STEP_HEADS,), out_shape=(jax.Shape...]
    convert_element_type x2 -> x0, local copies, waits for them, and re-layouts: 18.1 us -> none  [the longest x1 13.9 us: per_device(): pooled.astype(jnp.bfloat16)]
    all_to_all x1, waiting for transfers between devices: 28 us -> 11.7 us  [exchange(): return lax.all_to_all(x, AXES, split_axis=0, concat_axis=0, tiled=True)]
    unnamed x27 -> x9, local copies, waits for them, and re-layouts: 16.3 us -> 1.75 us
    slice x3 -> x0, local copies, waits for them, and re-layouts: 7.36 us -> none  [the longest x1 3.6 us: pair_grads(): q_head = query[:, head * width:(head + 1) * width].reshape(rows, group, DH)]
  transfers between devices with their start and end apart: 3 -> 1, of which waited for: 3 -> 1; matrix products, arithmetic and copies ran while one was open for 11% -> 2% of each run, Pallas kernels for 0% -> 0%
where the time goes in v1:
time: 122 us
  blocking collectives  67.5 us (55%)
  Pallas kernels  33.2 us (27%)
  waiting for transfers between devices  11.7 us (10%)
  starting transfers between devices  4.56 us (4%)
  local copies, waits for them, and re-layouts  2.91 us (2%)
  between operations  1.9 us (2%)
    all_to_all x3, blocking collectives, exchange(): return lax.all_to_all(x, AXES, split_axis=0, concat_axis=0, tiled=True)  67.5 us
    pallas_call x1, Pallas kernels, per_device(): pl.pallas_call(pair_kernel, grid=(H // STEP_HEADS,), out_shape=(jax.Shape...  23.6 us
    all_to_all x1, waiting for transfers between devices, exchange(): return lax.all_to_all(x, AXES, split_axis=0, concat_axis=0, tiled=True)  11.7 us
    all_to_all x1, starting transfers between devices, exchange(): return lax.all_to_all(x, AXES, split_axis=0, concat_axis=0, tiled=True)  4.56 us
    pallas_call x1, Pallas kernels, per_device(): pl.pallas_call(pool_kernel, out_shape=low, in_specs=[smem, smem, vmem], o...  2.89 us
  transfers between devices with their start and end apart: 1, of which 1 were waited for; matrix products, arithmetic and copies ran while one was open for 2% of the time, Pallas kernels for 0%

profile of v1, /device:TPU:1, one launch (start us, length us, event | category | flops | bytes accessed | tf_op | source)
XLA Modules:
  0.0 121.8 jit_solution(9008574126485293307)
XLA Ops:
  0.6 0.0 copy-start.3
  0.6 0.0 copy-start.2
  0.7 0.0 copy-start.1
  0.7 2.2 %spread.1 = bf16[128,4,640]{2,1,0:T(4,128)(2,1)} custom-call(bf16[640,256]{1,0:T(8,128)(2,1)} %k_ref.1, bf16[640,256]{1,0:T(8,128)(2,1)} %v_ref.1), custom_call_target="tpu_custom_call" | custom-call | tf_op jit(solution)/shard_map/spread/pallas_call | solution.py:142
  2.8 26.6 %all_to_all.20.in_ref = bf16[128,4,640]{2,1,0:T(4,128)(2,1)} all-to-all(bf16[128,4,640]{2,1,0:T(4,128)(2,1)} %spread.1), channel_id=1, replica_groups=mesh['grp'=16,'blk'=8] {'grp','blk'}, dimensions={0} | all-to-all | bytes 1310720 | tf_op jit(solution)/shard_map/all_to_all | solution.py:129
  29.4 2.4 %select.1 = bf16[128,4,640]{2,1,0:T(4,128)(2,1)} custom-call(s32[128]{0:T(128)} %held_ref.3, s32[128]{0:T(128)} %key_ref.3, bf16[128,4,640]{2,1,0:T(4,128)(2,1)} %all_to_all.20.in_ref), custom_call_target="tpu_custom_call" | custom-call | tf_op jit(solution)/shard_map/select/pallas_call | solution.py:146
  31.9 4.6 %all-to-all-start.1 = ((bf16[128,4,640]{2,1,0:T(4,128)(2,1)}), bf16[128,4,640]{2,1,0:T(4,128)(2,1)S(1)}, u32[]{:S(2)}, u32[]{:S(2)}) async-start(bf16[128,4,640]{2,1,0:T(4,128)(2,1)} %select.1), calls=%async_computation.1 | async-start | bytes 1310720 | tf_op jit(solution)/shard_map/all_to_all | solution.py:129
  36.4 0.0 copy-done.3
  36.4 0.6 dynamic_slice.8
  37.0 0.0 copy-done.2
  37.0 0.6 dynamic_slice.7
  37.6 0.0 copy-done.1
  37.6 0.9 copy.11.norm_ref
  39.7 11.7 %all-to-all-done.1.kv_ref = bf16[128,4,640]{2,1,0:T(4,128)(2,1)S(1)} async-done(((bf16[128,4,640]{2,1,0:T(4,128)(2,1)}), bf16[128,4,640]{2,1,0:T(4,128)(2,1)S(1)}, u32[]{:S(2)}, u32[]{:S(2)}) %all-to-all-start.1) | async-done | bytes 655392 | tf_op jit(solution)/shard_map/all_to_all | solution.py:129
  51.4 0.0 copy-start
  51.4 0.8 copy-done
  52.3 23.6 %pair.1 = (bf16[640,2048]{1,0:T(8,128)(2,1)}, bf16[128,4,640]{2,1,0:T(4,128)(2,1)}) custom-call(s32[1]{0:T(128)S(6)} %select_n.10.off_ref, bf16[640,2048]{1,0:T(8,128)(2,1)} %q_ref.1, bf16[640,2048]{1,0:T(8,128)(2,1)} %do_ref.1, bf16[640,2048]{1,0:T(8,128)(2,1)} %o_ref.1, f32[640,16]{1,0:T(8,128)} %copy.11.norm_ref, bf16[128,4,640]{2,1,0:T(4,128)(2,1)} %copy-done), custom_call_target="tpu_custom_call" | custom-call | tf_op jit(solution)/shard_map/pair/pallas_call | solution.py:161
  75.9 20.5 %all_to_all.21.in_ref = bf16[128,4,640]{2,1,0:T(4,128)(2,1)} all-to-all(bf16[128,4,640]{2,1,0:T(4,128)(2,1)} %get-tuple-element.8), channel_id=1, replica_groups=mesh['grp'=16,'blk'=8] {'grp','blk'}, dimensions={0} | all-to-all | bytes 1310720 | tf_op jit(solution)/shard_map/all_to_all | solution.py:129
  96.4 2.9 %pool.1 = bf16[128,4,640]{2,1,0:T(4,128)(2,1)} custom-call(s32[128]{0:T(128)} %held_ref.3, s32[128]{0:T(128)} %key_ref.3, bf16[128,4,640]{2,1,0:T(4,128)(2,1)} %all_to_all.21.in_ref), custom_call_target="tpu_custom_call" | custom-call | tf_op jit(solution)/shard_map/pool/pallas_call | solution.py:184
  99.2 20.5 %all_to_all.22.in_ref = bf16[128,4,640]{2,1,0:T(4,128)(2,1)} all-to-all(bf16[128,4,640]{2,1,0:T(4,128)(2,1)} %pool.1), channel_id=1, replica_groups=mesh['grp'=16,'blk'=8] {'grp','blk'}, dimensions={0} | all-to-all | bytes 1310720 | tf_op jit(solution)/shard_map/all_to_all | solution.py:129
  119.7 2.1 %finish.1 = (bf16[640,256]{1,0:T(8,128)(2,1)}, bf16[640,256]{1,0:T(8,128)(2,1)}) custom-call(bf16[128,4,640]{2,1,0:T(4,128)(2,1)} %all_to_all.22.in_ref), custom_call_target="tpu_custom_call" | custom-call | tf_op jit(solution)/shard_map/finish/pallas_call | solution.py:193
Async XLA Ops:
  0.6 35.8 %copy-start.3 = (s32[128]{0:T(128)S(1)}, s32[128]{0:T(128)}, u32[]{:S(2)}) copy-start(s32[128]{0:T(128)} %key_ref.3) | copy-start | bytes 1540
  0.6 36.4 %copy-start.2 = (s32[128]{0:T(128)S(1)}, s32[128]{0:T(128)}, u32[]{:S(2)}) copy-start(s32[128]{0:T(128)} %held_ref.3) | copy-start | bytes 1540
  0.7 36.9 %copy-start.1 = (f32[640,16]{0,1:T(8,128)S(1)}, f32[640,16]{0,1:T(8,128)}, u32[]{:S(2)}) copy-start(f32[640,16]{0,1:T(8,128)} %param.13) | copy-start | bytes 122884
  31.9 19.6 %all-to-all-start.1 = ((bf16[128,4,640]{2,1,0:T(4,128)(2,1)}), bf16[128,4,640]{2,1,0:T(4,128)(2,1)S(1)}, u32[]{:S(2)}, u32[]{:S(2)}) async-start(bf16[128,4,640]{2,1,0:T(4,128)(2,1)} %select.1), calls=%async_computation.1 | async-start | bytes 1310720 | tf_op jit(solution)/shard_map/all_to_all | solution.py:129
  51.4 0.8 copy-start

commit v2 on v1

v2 whole, which is shorter than its diff:
```python
import functools

import jax
import jax.numpy as jnp
from jax import lax
from jax.experimental import pallas as pl
from jax.experimental.pallas import tpu as pltpu
from jax.sharding import PartitionSpec as P

H = 16
KVH = 2
DH = 128
GROUP = H // KVH
AXES = ("grp", "blk")
SCALE = DH ** (-0.5)
LOG2E = 1.4426950408889634
STEP_HEADS = 2
TERMS = 3
SMALL = pltpu.CompilerParams(vmem_limit_bytes=8 * 1024 * 1024)
BIG_LIMIT = 125 * 512 * 1024
FULL_LIMIT = 67043328


def spread_kernel(k_hbm, v_hbm, out_ref, k_ref, v_ref, sems):
    parts, depth, rows = out_ref.shape
    half = parts // 2
    copies = [
        pltpu.make_async_copy(k_hbm, k_ref, sems.at[0]),
        pltpu.make_async_copy(v_hbm, v_ref, sems.at[1]),
    ]
    for copy in copies:
        copy.start()
    for at, ref in enumerate((k_ref, v_ref)):
        copies[at].wait()
        out_ref[at * half : (at + 1) * half] = ref[...].T.reshape(half, depth, rows)


def prep_kernel(
    own_ref, held_ref, key_ref, norm_ref, q_ref, do_ref, o_ref,
    holder_ref, off_ref, aux_ref, q_t_ref, do_t_ref, pos_ref, delta_ref,
):
    step = pl.program_id(0)
    rows = q_ref.shape[0]
    count = held_ref.shape[0]

    @pl.when(step == 0)
    def _():
        def put(e, carry):
            pos_ref[held_ref[e]] = e
            return carry

        def look(d, carry):
            holder_ref[d] = pos_ref[key_ref[d]]
            return carry

        lax.fori_loop(0, count, put, 0, unroll=8)
        lax.fori_loop(0, count, look, 0, unroll=8)
        own = own_ref[0]
        off_ref[0] = jnp.where(held_ref[own] == key_ref[own], 0, rows)
        delta_ref[...] = jnp.zeros_like(delta_ref)

    q_t_ref[...] = q_ref[...].T
    do_t_ref[...] = do_ref[...].T
    lanes = lax.broadcasted_iota(jnp.int32, delta_ref.shape, 1)
    delta = delta_ref[...]
    for sub in range(STEP_HEADS):
        cols = slice(sub * DH, (sub + 1) * DH)
        both = do_ref[:, cols].astype(jnp.float32) * o_ref[:, cols].astype(jnp.float32)
        one = jnp.sum(both, axis=1, keepdims=True)
        delta = jnp.where(lanes == step * STEP_HEADS + sub, one, delta)
    delta_ref[...] = delta

    @pl.when(step == pl.num_programs(0) - 1)
    def _():
        norms = norm_ref[...] * DH**0.5
        norms = jnp.concatenate([norms, jnp.zeros((rows, DH - H), jnp.float32)], axis=1)
        total = jnp.zeros((rows, DH), jnp.float32)
        for at, left in enumerate((norms, delta_ref[...])):
            for term in range(TERMS):
                part = left.astype(jnp.bfloat16).astype(jnp.float32)
                left = left - part
                shift = (at * TERMS + term) * H
                total = total + (pltpu.roll(part, shift, 1) if shift else part)
        aux_ref[...] = total.astype(aux_ref.dtype)


def select_kernel(holder_ref, in_ref, out_ref):
    def move(d, carry):
        out_ref[d] = in_ref[holder_ref[d]]
        return carry

    lax.fori_loop(0, holder_ref.shape[0], move, 0, unroll=8)


def pool_kernel(holder_ref, in_ref, out_ref, total_ref):
    total_ref[...] = jnp.zeros_like(total_ref)

    def add(d, carry):
        at = holder_ref[d]
        total_ref[at] = total_ref[at] + in_ref[d].astype(jnp.float32)
        return carry

    lax.fori_loop(0, holder_ref.shape[0], add, 0, unroll=8)
    out_ref[...] = total_ref[...].astype(out_ref.dtype)


def finish_kernel(in_ref, k_ref, v_ref):
    parts, depth, rows = in_ref.shape
    half = parts // 2
    for at, ref in enumerate((k_ref, v_ref)):
        flat = in_ref[at * half : (at + 1) * half].reshape(half * depth, rows)
        ref[...] = flat.T


def picker(which, head):
    row = lax.broadcasted_iota(jnp.int32, (DH, DH), 0) - which * TERMS * H
    hit = (row >= 0) & (row < TERMS * H) & (row % H == head)
    return jnp.where(hit, -1.0, 0.0).astype(jnp.bfloat16)


def pair_kernel(
    off_ref, q_ref, do_ref, q_t_ref, do_t_ref, aux_ref, kv_ref, ds_ref, term_ref,
    flat_ref, bias_ref, dk_ref, dv_ref,
):
    step = pl.program_id(0)
    per_group = GROUP // STEP_HEADS
    c = step // per_group
    at = step % per_group
    rows = q_ref.shape[0]
    depth = kv_ref.shape[1]
    pieces = DH // depth

    @pl.when(step == 0)
    def _():
        flat_ref[...] = kv_ref[...].reshape(flat_ref.shape)
        limit = lax.broadcasted_iota(jnp.int32, (rows, rows), 0) + off_ref[0]
        col = lax.broadcasted_iota(jnp.int32, (rows, rows), 1)
        bias_ref[...] = jnp.where(col <= limit, 0.0, -jnp.inf)

    @pl.when(at == 0)
    def _():
        dk_ref[...] = jnp.zeros_like(dk_ref)
        dv_ref[...] = jnp.zeros_like(dv_ref)

    k_t = flat_ref[pl.ds(pl.multiple_of(c * DH, DH), DH), :]
    v_t = flat_ref[pl.ds(pl.multiple_of((KVH + c) * DH, DH), DH), :]
    aux = aux_ref[...]

    def shifted(left, right, which, head):
        tail = jnp.concatenate([picker(which, head)] * (rows // DH), axis=1)
        return jnp.dot(
            jnp.concatenate([left, aux], axis=1),
            jnp.concatenate([right, tail], axis=0),
            preferred_element_type=jnp.float32,
        )

    for sub in range(STEP_HEADS):
        cols = slice(sub * DH, (sub + 1) * DH)
        head = step * STEP_HEADS + sub
        s = shifted(q_ref[:, cols], k_t, 0, head)
        dp = shifted(do_ref[:, cols], v_t, 1, head)
        p = jnp.exp2(s * (DH**-0.5 * LOG2E) + bias_ref[...])
        ds = (p * dp).astype(jnp.bfloat16)
        ds_ref[sub] = ds
        dv_ref[...] += jnp.dot(
            do_t_ref[cols, :], p.astype(jnp.bfloat16), preferred_element_type=jnp.float32
        )
        dk_ref[...] += jnp.dot(q_t_ref[cols, :], ds, preferred_element_type=jnp.float32)

    @pl.when(at == per_group - 1)
    def _():
        low_k = (dk_ref[...] * SCALE).astype(term_ref.dtype)
        low_v = dv_ref[...].astype(term_ref.dtype)
        term_ref[pl.ds(c * pieces, pieces)] = low_k.reshape(pieces, depth, rows)
        term_ref[pl.ds((KVH + c) * pieces, pieces)] = low_v.reshape(pieces, depth, rows)


def query_kernel(ds_ref, kv_ref, dq_ref, flat_ref, k_ref):
    step = pl.program_id(0)
    per_group = GROUP // STEP_HEADS
    c = step // per_group

    @pl.when(step == 0)
    def _():
        flat_ref[...] = kv_ref[: kv_ref.shape[0] // 2].reshape(flat_ref.shape)

    @pl.when(step % per_group == 0)
    def _():
        k_ref[...] = flat_ref[pl.ds(pl.multiple_of(c * DH, DH), DH), :].T

    for sub in range(STEP_HEADS):
        dq = jnp.dot(ds_ref[sub], k_ref[...], preferred_element_type=jnp.float32) * SCALE
        dq_ref[:, sub * DH : (sub + 1) * DH] = dq.astype(dq_ref.dtype)


def exchange(x):
    return lax.all_to_all(x, AXES, split_axis=0, concat_axis=0, tiled=True)


def cost(flops, bytes_accessed):
    return pl.CostEstimate(flops=flops, bytes_accessed=bytes_accessed, transcendentals=0)


def per_device(queries, key_rows, value_rows, out_grad, attn_out, log_norm, held_block, key_block):
    count = lax.axis_size("grp") * lax.axis_size("blk")
    own = lax.axis_index("grp") * lax.axis_size("blk") + lax.axis_index("blk")
    rows = queries.shape[0]
    depth = 2 * KVH * DH // count
    piece = (count, depth, rows)
    low = jax.ShapeDtypeStruct(piece, jnp.bfloat16)
    vmem = pl.BlockSpec(memory_space=pltpu.VMEM)
    smem = pl.BlockSpec(memory_space=pltpu.SMEM)
    hbm = pl.BlockSpec(memory_space=pltpu.HBM)
    width = STEP_HEADS * DH
    steps = H // STEP_HEADS
    wide = pl.BlockSpec((rows, width), lambda s: (0, s))
    tall = pl.BlockSpec((width, rows), lambda s: (s, 0))
    whole = pl.BlockSpec(piece, lambda s: (0, 0, 0))
    aux_spec = pl.BlockSpec((rows, DH), lambda s: (0, 0))
    big = pltpu.CompilerParams(
        dimension_semantics=("arbitrary",), vmem_limit_bytes=BIG_LIMIT
    )
    matmul = 2 * H * rows * rows * DH
    wide_bytes = 2 * rows * H * DH

    spread = pl.pallas_call(
        spread_kernel,
        out_shape=low,
        in_specs=[hbm] * 2,
        out_specs=vmem,
        scratch_shapes=[
            pltpu.VMEM(key_rows.shape, jnp.bfloat16),
            pltpu.VMEM(value_rows.shape, jnp.bfloat16),
            pltpu.SemaphoreType.DMA((2,)),
        ],
        compiler_params=pltpu.CompilerParams(vmem_limit_bytes=FULL_LIMIT),
        name="spread",
    )(key_rows, value_rows)
    gathered = exchange(spread)
    turned = jax.ShapeDtypeStruct((H * DH, rows), jnp.bfloat16)
    holder, off, aux, q_t, do_t = pl.pallas_call(
        prep_kernel,
        grid=(steps,),
        out_shape=(
            jax.ShapeDtypeStruct((count,), jnp.int32),
            jax.ShapeDtypeStruct((1,), jnp.int32),
            jax.ShapeDtypeStruct((rows, DH), jnp.bfloat16),
            turned,
            turned,
        ),
        in_specs=[
            smem, smem, smem, pl.BlockSpec(log_norm.shape, lambda s: (0, 0)), wide, wide, wide,
        ],
        out_specs=(smem, smem, aux_spec, tall, tall),
        scratch_shapes=[pltpu.SMEM((count,), jnp.int32), pltpu.VMEM((rows, DH), jnp.float32)],
        compiler_params=big,
        cost_estimate=cost(matmul // 2, 5 * wide_bytes),
        name="prep",
    )(own.reshape(1).astype(jnp.int32), held_block, key_block, log_norm, queries, out_grad, attn_out)
    chosen = pl.pallas_call(
        select_kernel,
        out_shape=low,
        in_specs=[smem, vmem],
        out_specs=vmem,
        compiler_params=SMALL,
        name="select",
    )(holder, gathered)
    kv = exchange(chosen)

    kept = pl.BlockSpec((STEP_HEADS, rows, rows), lambda s: (s, 0, 0))
    ds, term = pl.pallas_call(
        pair_kernel,
        grid=(steps,),
        out_shape=(jax.ShapeDtypeStruct((H, rows, rows), jnp.bfloat16), low),
        in_specs=[smem, wide, wide, tall, tall, aux_spec, whole],
        out_specs=(kept, whole),
        scratch_shapes=[
            pltpu.VMEM((2 * KVH * DH, rows), jnp.bfloat16),
            pltpu.VMEM((rows, rows), jnp.float32),
            pltpu.VMEM((DH, rows), jnp.float32),
            pltpu.VMEM((DH, rows), jnp.float32),
        ],
        compiler_params=big,
        cost_estimate=cost(4 * matmul, 4 * wide_bytes + 2 * H * rows * rows),
        name="pair",
    )(off, queries, out_grad, q_t, do_t, aux, kv)
    returned = exchange(term)
    query_grad = pl.pallas_call(
        query_kernel,
        grid=(steps,),
        out_shape=jax.ShapeDtypeStruct(queries.shape, jnp.bfloat16),
        in_specs=[kept, whole],
        out_specs=wide,
        scratch_shapes=[
            pltpu.VMEM((KVH * DH, rows), jnp.bfloat16),
            pltpu.VMEM((rows, DH), jnp.bfloat16),
        ],
        compiler_params=big,
        cost_estimate=cost(matmul, wide_bytes + 2 * H * rows * rows),
        name="query",
    )(ds, kv)
    pooled = pl.pallas_call(
        pool_kernel,
        out_shape=low,
        in_specs=[smem, vmem],
        out_specs=vmem,
        scratch_shapes=[pltpu.VMEM(piece, jnp.float32)],
        compiler_params=SMALL,
        name="pool",
    )(holder, returned)
    home = exchange(pooled)
    key_grad, value_grad = pl.pallas_call(
        finish_kernel,
        out_shape=(
            jax.ShapeDtypeStruct(key_rows.shape, jnp.bfloat16),
            jax.ShapeDtypeStruct(value_rows.shape, jnp.bfloat16),
        ),
        in_specs=[vmem],
        out_specs=(vmem, vmem),
        compiler_params=SMALL,
        name="finish",
    )(home)
    return (query_grad, key_grad, value_grad)


def solution(mesh):
    rows = P(AXES, None)
    return jax.shard_map(
        per_device,
        mesh=mesh,
        in_specs=(rows,) * 6 + (P(), P()),
        out_specs=(rows, rows, rows),
        check_vma=False,
    )
```

time: 122 us -> 115 us (0.943)
  blocking collectives: 67.5 us -> 41.2 us
  Pallas kernels: 33.2 us -> 45.7 us
  starting transfers between devices: 4.56 us -> 16.1 us
  waiting for transfers between devices: 11.7 us -> 7.79 us
  between operations: 1.9 us -> 0.67 us
    all_to_all x3 -> x2, blocking collectives: 67.5 us -> 41.2 us  [exchange(): return lax.all_to_all(x, AXES, split_axis=0, concat_axis=0, tiled=True)]
    pallas_call x4 -> x6, Pallas kernels: 31.1 us -> 44.7 us  [the longest x1 19.2 us: per_device(): pl.pallas_call(pair_kernel, grid=(steps,), out_shape=(jax.ShapeDtypeStruc...]
    all_to_all x1 -> x2, starting transfers between devices: 4.56 us -> 16.1 us  [exchange(): return lax.all_to_all(x, AXES, split_axis=0, concat_axis=0, tiled=True)]
    all_to_all x1 -> x2, waiting for transfers between devices: 11.7 us -> 7.79 us  [exchange(): return lax.all_to_all(x, AXES, split_axis=0, concat_axis=0, tiled=True)]
  transfers between devices with their start and end apart: 1 -> 2, of which waited for: 1 -> 2; matrix products, arithmetic and copies ran while one was open for 2% -> 1% of each run, Pallas kernels for 0% -> 18%
where the time goes in v2:
time: 115 us; the launch traced here: 114 us
  Pallas kernels  45.7 us (40%)
  blocking collectives  41.2 us (36%)
  starting transfers between devices  16.1 us (14%)
  waiting for transfers between devices  7.79 us (7%)
  local copies, waits for them, and re-layouts  2.32 us (2%)
    all_to_all x2, blocking collectives, exchange(): return lax.all_to_all(x, AXES, split_axis=0, concat_axis=0, tiled=True)  41.2 us
    pallas_call x1, Pallas kernels, per_device(): pl.pallas_call(pair_kernel, grid=(steps,), out_shape=(jax.ShapeDtypeStruc...  19.2 us
    all_to_all x2, starting transfers between devices, exchange(): return lax.all_to_all(x, AXES, split_axis=0, concat_axis=0, tiled=True)  16.1 us
    pallas_call x1, Pallas kernels, per_device(): pl.pallas_call(query_kernel, grid=(steps,), out_shape=jax.ShapeDtypeStruc...  10.5 us
    pallas_call x1, Pallas kernels, per_device(): pl.pallas_call(prep_kernel, grid=(steps,), out_shape=(jax.ShapeDtypeStruc...  10.1 us
    all_to_all x2, waiting for transfers between devices, exchange(): return lax.all_to_all(x, AXES, split_axis=0, concat_axis=0, tiled=True)  7.79 us
    unnamed x5, local copies, waits for them, and re-layouts  2.32 us
  transfers between devices with their start and end apart: 2, of which 2 were waited for; matrix products, arithmetic and copies ran while one was open for 1% of the time, Pallas kernels for 18%

profile of v2, /device:TPU:1, one launch (start us, length us, event | category | flops | bytes accessed | tf_op | source)
XLA Modules:
  0.0 113.7 jit_solution(3207101253604787250)
XLA Ops:
  0.6 2.1 %spread.1 = bf16[128,4,640]{2,1,0:T(4,128)(2,1)} custom-call(bf16[640,256]{1,0:T(8,128)(2,1)} %k_hbm.1, bf16[640,256]{1,0:T(8,128)(2,1)} %v_hbm.1), custom_call_target="tpu_custom_call" | custom-call | tf_op jit(solution)/shard_map/spread/pallas_call | solution.py:226
  2.8 11.5 %all-to-all-start = ((bf16[128,4,640]{2,1,0:T(4,128)(2,1)}), bf16[128,4,640]{2,1,0:T(4,128)(2,1)S(1)}, u32[]{:S(2)}, u32[]{:S(2)}) async-start(bf16[128,4,640]{2,1,0:T(4,128)(2,1)} %spread.1), calls=%async_computation | async-start | bytes 1310720 | tf_op jit(solution)/shard_map/all_to_all | solution.py:197
  14.3 1.7 %copy.11.norm_ref = f32[640,16]{1,0:T(8,128)} copy(f32[640,16]{0,1:T(8,128)} %param.13) | data formatting | bytes 81920 | tf_op args[5]
  15.9 10.1 %prep.1 = (s32[128]{0:T(128)}, s32[1]{0:T(128)}, bf16[640,128]{1,0:T(8,128)(2,1)}, bf16[2048,640]{1,0:T(8,128)(2,1)}, bf16[2048,640]{1,0:T(8,128)(2,1)}) custom-call(s32[1]{0:T(128)} %bitcast.own_ref, s32[128]{0:T(128)} %held_ref.1, s32[128]{0:T(128)} %key_ref.1, f32[640,16]{1,0:T(8,128)} %copy.11.norm_ref, bf16[640,2048]{1,0:T(8,128)(2,1)} %q_ref.3, ...), custom_call_target="tpu_custom_call" | custom-call | flops 838860800 | bytes 13107200 | tf_op jit(solution)/shard_map/prep/pallas_call | solution.py:241
  26.0 3.3 %all-to-all-done.in_ref = bf16[128,4,640]{2,1,0:T(4,128)(2,1)S(1)} async-done(((bf16[128,4,640]{2,1,0:T(4,128)(2,1)}), bf16[128,4,640]{2,1,0:T(4,128)(2,1)S(1)}, u32[]{:S(2)}, u32[]{:S(2)}) %all-to-all-start) | async-done | bytes 655392 | tf_op jit(solution)/shard_map/all_to_all | solution.py:197
  29.3 0.0 copy-start
  29.3 0.6 copy-done
  29.9 0.8 select.1
  30.7 21.4 %all_to_all.20.kv_ref = bf16[128,4,640]{2,1,0:T(4,128)(2,1)} all-to-all(bf16[128,4,640]{2,1,0:T(4,128)(2,1)S(1)} %select.1), channel_id=1, replica_groups=mesh['grp'=16,'blk'=8] {'grp','blk'}, dimensions={0} | all-to-all | bytes 1310720 | tf_op jit(solution)/shard_map/all_to_all | solution.py:197
  52.1 0.0 copy-start.1
  52.1 19.2 %pair.1 = (bf16[16,640,640]{2,1,0:T(8,128)(2,1)}, bf16[128,4,640]{2,1,0:T(4,128)(2,1)}) custom-call(s32[1]{0:T(128)} %get-tuple-element.12.off_ref, bf16[640,2048]{1,0:T(8,128)(2,1)} %q_ref.3, bf16[640,2048]{1,0:T(8,128)(2,1)} %do_ref.3, bf16[2048,640]{1,0:T(8,128)(2,1)} %get-tuple-element.13.q_t_ref, bf16[2048,640]{1,0:T(8,128)(2,1)} %get-tuple-element.14.do_t_ref, ...), custom_call_target="tpu_custom_call" | custom-call | flops 6710886400 | bytes 23592960 | tf_op jit(solution)/shard_map/pair/pallas_call | solution.py:271
  71.3 19.8 %all_to_all.21.in_ref = bf16[128,4,640]{2,1,0:T(4,128)(2,1)S(1)} all-to-all(bf16[128,4,640]{2,1,0:T(4,128)(2,1)} %get-tuple-element.18), channel_id=1, replica_groups=mesh['grp'=16,'blk'=8] {'grp','blk'}, dimensions={0} | all-to-all | bytes 1310720 | tf_op jit(solution)/shard_map/all_to_all | solution.py:197
  91.1 0.0 copy-done.1
  91.1 2.1 %pool.1 = bf16[128,4,640]{2,1,0:T(4,128)(2,1)} custom-call(s32[128]{0:T(128)S(1)} %copy-done.1, bf16[128,4,640]{2,1,0:T(4,128)(2,1)S(1)} %all_to_all.21.in_ref), custom_call_target="tpu_custom_call" | custom-call | tf_op jit(solution)/shard_map/pool/pallas_call | solution.py:302
  93.1 4.6 %all-to-all-start.3 = ((bf16[128,4,640]{2,1,0:T(4,128)(2,1)}), bf16[128,4,640]{2,1,0:T(4,128)(2,1)S(1)}, u32[]{:S(2)}, u32[]{:S(2)}) async-start(bf16[128,4,640]{2,1,0:T(4,128)(2,1)} %pool.1), calls=%async_computation.3 | async-start | bytes 1310720 | tf_op jit(solution)/shard_map/all_to_all | solution.py:197
  97.7 10.5 %query.1 = bf16[640,2048]{1,0:T(8,128)(2,1)} custom-call(bf16[16,640,640]{2,1,0:T(8,128)(2,1)} %get-tuple-element.17.ds_ref, bf16[128,4,640]{2,1,0:T(4,128)(2,1)} %all_to_all.20.kv_ref), custom_call_target="tpu_custom_call" | custom-call | flops 1677721600 | bytes 15728640 | tf_op jit(solution)/shard_map/query/pallas_call | solution.py:288
  108.2 4.5 %all-to-all-done.3.in_ref = bf16[128,4,640]{2,1,0:T(4,128)(2,1)S(1)} async-done(((bf16[128,4,640]{2,1,0:T(4,128)(2,1)}), bf16[128,4,640]{2,1,0:T(4,128)(2,1)S(1)}, u32[]{:S(2)}, u32[]{:S(2)}) %all-to-all-start.3) | async-done | bytes 655392 | tf_op jit(solution)/shard_map/all_to_all | solution.py:197
  112.7 1.0 finish.1
Async XLA Ops:
  2.8 26.5 %all-to-all-start = ((bf16[128,4,640]{2,1,0:T(4,128)(2,1)}), bf16[128,4,640]{2,1,0:T(4,128)(2,1)S(1)}, u32[]{:S(2)}, u32[]{:S(2)}) async-start(bf16[128,4,640]{2,1,0:T(4,128)(2,1)} %spread.1), calls=%async_computation | async-start | bytes 1310720 | tf_op jit(solution)/shard_map/all_to_all | solution.py:197
  29.3 0.6 copy-start
  52.1 38.9 %copy-start.1 = (s32[128]{0:T(128)S(1)}, s32[128]{0:T(128)}, u32[]{:S(2)}) copy-start(s32[128]{0:T(128)} %get-tuple-element.16.holder_ref) | copy-start | bytes 1540
  93.1 19.6 %all-to-all-start.3 = ((bf16[128,4,640]{2,1,0:T(4,128)(2,1)}), bf16[128,4,640]{2,1,0:T(4,128)(2,1)S(1)}, u32[]{:S(2)}, u32[]{:S(2)}) async-start(bf16[128,4,640]{2,1,0:T(4,128)(2,1)} %pool.1), calls=%async_computation.3 | async-start | bytes 1310720 | tf_op jit(solution)/shard_map/all_to_all | solution.py:197

commit v3 on v2

--- a/solution.py
+++ b/solution.py
@@ -14,9 +14,10 @@
 AXES = ("grp", "blk")
 SCALE = DH ** (-0.5)
 LOG2E = 1.4426950408889634
-STEP_HEADS = 2
+STEP_HEADS = 4
 TERMS = 3
 SMALL = pltpu.CompilerParams(vmem_limit_bytes=8 * 1024 * 1024)
+BLOCK = 640
 BIG_LIMIT = 125 * 512 * 1024
 FULL_LIMIT = 67043328
 
@@ -35,32 +36,32 @@
         out_ref[at * half : (at + 1) * half] = ref[...].T.reshape(half, depth, rows)
 
 
+def table_kernel(own_ref, held_ref, key_ref, holder_ref, off_ref, pos_ref):
+    def put(e, carry):
+        pos_ref[held_ref[e]] = e
+        return carry
+
+    def look(d, carry):
+        holder_ref[d] = pos_ref[key_ref[d]]
+        return carry
+
+    count = held_ref.shape[0]
+    lax.fori_loop(0, count, put, 0, unroll=8)
+    lax.fori_loop(0, count, look, 0, unroll=8)
+    own = own_ref[0]
+    off_ref[0] = jnp.where(held_ref[own] == key_ref[own], 0, BLOCK)
+
+
 def prep_kernel(
-    own_ref, held_ref, key_ref, norm_ref, q_ref, do_ref, o_ref,
-    holder_ref, off_ref, aux_ref, q_t_ref, do_t_ref, pos_ref, delta_ref,
+    norm_ref, do_ref, o_ref, aux_ref, delta_ref,
 ):
     step = pl.program_id(0)
-    rows = q_ref.shape[0]
-    count = held_ref.shape[0]
+    rows = do_ref.shape[0]
 
     @pl.when(step == 0)
     def _():
-        def put(e, carry):
-            pos_ref[held_ref[e]] = e
-            return carry
-
-        def look(d, carry):
-            holder_ref[d] = pos_ref[key_ref[d]]
-            return carry
-
-        lax.fori_loop(0, count, put, 0, unroll=8)
-        lax.fori_loop(0, count, look, 0, unroll=8)
-        own = own_ref[0]
-        off_ref[0] = jnp.where(held_ref[own] == key_ref[own], 0, rows)
         delta_ref[...] = jnp.zeros_like(delta_ref)
 
-    q_t_ref[...] = q_ref[...].T
-    do_t_ref[...] = do_ref[...].T
     lanes = lax.broadcasted_iota(jnp.int32, delta_ref.shape, 1)
     delta = delta_ref[...]
     for sub in range(STEP_HEADS):
@@ -119,7 +120,7 @@
 
 
 def pair_kernel(
-    off_ref, q_ref, do_ref, q_t_ref, do_t_ref, aux_ref, kv_ref, ds_ref, term_ref,
+    off_ref, q_ref, do_ref, aux_ref, kv_ref, ds_ref, term_ref, keys_ref,
     flat_ref, bias_ref, dk_ref, dv_ref,
 ):
     step = pl.program_id(0)
@@ -133,6 +134,7 @@
     @pl.when(step == 0)
     def _():
         flat_ref[...] = kv_ref[...].reshape(flat_ref.shape)
+        keys_ref[...] = flat_ref[: KVH * DH, :]
         limit = lax.broadcasted_iota(jnp.int32, (rows, rows), 0) + off_ref[0]
         col = lax.broadcasted_iota(jnp.int32, (rows, rows), 1)
         bias_ref[...] = jnp.where(col <= limit, 0.0, -jnp.inf)
@@ -163,9 +165,9 @@
         ds = (p * dp).astype(jnp.bfloat16)
         ds_ref[sub] = ds
         dv_ref[...] += jnp.dot(
-            do_t_ref[cols, :], p.astype(jnp.bfloat16), preferred_element_type=jnp.float32
+            do_ref[:, cols].T, p.astype(jnp.bfloat16), preferred_element_type=jnp.float32
         )
-        dk_ref[...] += jnp.dot(q_t_ref[cols, :], ds, preferred_element_type=jnp.float32)
+        dk_ref[...] += jnp.dot(q_ref[:, cols].T, ds, preferred_element_type=jnp.float32)
 
     @pl.when(at == per_group - 1)
     def _():
@@ -175,18 +177,14 @@
         term_ref[pl.ds((KVH + c) * pieces, pieces)] = low_v.reshape(pieces, depth, rows)
 
 
-def query_kernel(ds_ref, kv_ref, dq_ref, flat_ref, k_ref):
+def query_kernel(ds_ref, keys_ref, dq_ref, k_ref):
     step = pl.program_id(0)
     per_group = GROUP // STEP_HEADS
     c = step // per_group
 
-    @pl.when(step == 0)
-    def _():
-        flat_ref[...] = kv_ref[: kv_ref.shape[0] // 2].reshape(flat_ref.shape)
-
     @pl.when(step % per_group == 0)
     def _():
-        k_ref[...] = flat_ref[pl.ds(pl.multiple_of(c * DH, DH), DH), :].T
+        k_ref[...] = keys_ref[pl.ds(pl.multiple_of(c * DH, DH), DH), :].T
 
     for sub in range(STEP_HEADS):
         dq = jnp.dot(ds_ref[sub], k_ref[...], preferred_element_type=jnp.float32) * SCALE
@@ -214,7 +212,7 @@
     width = STEP_HEADS * DH
     steps = H // STEP_HEADS
     wide = pl.BlockSpec((rows, width), lambda s: (0, s))
-    tall = pl.BlockSpec((width, rows), lambda s: (s, 0))
+    keys_spec = pl.BlockSpec((KVH * DH, rows), lambda s: (0, 0))
     whole = pl.BlockSpec(piece, lambda s: (0, 0, 0))
     aux_spec = pl.BlockSpec((rows, DH), lambda s: (0, 0))
     big = pltpu.CompilerParams(
@@ -237,26 +235,30 @@
         name="spread",
     )(key_rows, value_rows)
     gathered = exchange(spread)
-    turned = jax.ShapeDtypeStruct((H * DH, rows), jnp.bfloat16)
-    holder, off, aux, q_t, do_t = pl.pallas_call(
-        prep_kernel,
-        grid=(steps,),
+    holder, off = pl.pallas_call(
+        table_kernel,
         out_shape=(
             jax.ShapeDtypeStruct((count,), jnp.int32),
             jax.ShapeDtypeStruct((1,), jnp.int32),
-            jax.ShapeDtypeStruct((rows, DH), jnp.bfloat16),
-            turned,
-            turned,
         ),
-        in_specs=[
-            smem, smem, smem, pl.BlockSpec(log_norm.shape, lambda s: (0, 0)), wide, wide, wide,
-        ],
-        out_specs=(smem, smem, aux_spec, tall, tall),
-        scratch_shapes=[pltpu.SMEM((count,), jnp.int32), pltpu.VMEM((rows, DH), jnp.float32)],
+        in_specs=[smem, smem, smem],
+        out_specs=(smem, smem),
+        scratch_shapes=[pltpu.SMEM((count,), jnp.int32)],
+        compiler_params=SMALL,
+        cost_estimate=cost(2**20, 2**12),
+        name="table",
+    )(own.reshape(1).astype(jnp.int32), held_block, key_block)
+    aux = pl.pallas_call(
+        prep_kernel,
+        grid=(steps,),
+        out_shape=jax.ShapeDtypeStruct((rows, DH), jnp.bfloat16),
+        in_specs=[pl.BlockSpec(log_norm.shape, lambda s: (0, 0)), wide, wide],
+        out_specs=aux_spec,
+        scratch_shapes=[pltpu.VMEM((rows, DH), jnp.float32)],
         compiler_params=big,
-        cost_estimate=cost(matmul // 2, 5 * wide_bytes),
+        cost_estimate=cost(matmul // 2, 2 * wide_bytes),
         name="prep",
-    )(own.reshape(1).astype(jnp.int32), held_block, key_block, log_norm, queries, out_grad, attn_out)
+    )(log_norm, out_grad, attn_out)
     chosen = pl.pallas_call(
         select_kernel,
         out_shape=low,
@@ -268,12 +270,16 @@
     kv = exchange(chosen)
 
     kept = pl.BlockSpec((STEP_HEADS, rows, rows), lambda s: (s, 0, 0))
-    ds, term = pl.pallas_call(
+    ds, term, keys = pl.pallas_call(
         pair_kernel,
         grid=(steps,),
-        out_shape=(jax.ShapeDtypeStruct((H, rows, rows), jnp.bfloat16), low),
-        in_specs=[smem, wide, wide, tall, tall, aux_spec, whole],
-        out_specs=(kept, whole),
+        out_shape=(
+            jax.ShapeDtypeStruct((H, rows, rows), jnp.bfloat16),
+            low,
+            jax.ShapeDtypeStruct((KVH * DH, rows), jnp.bfloat16),
+        ),
+        in_specs=[smem, wide, wide, aux_spec, whole],
+        out_specs=(kept, whole, keys_spec),
         scratch_shapes=[
             pltpu.VMEM((2 * KVH * DH, rows), jnp.bfloat16),
             pltpu.VMEM((rows, rows), jnp.float32),
@@ -283,22 +289,20 @@
         compiler_params=big,
         cost_estimate=cost(4 * matmul, 4 * wide_bytes + 2 * H * rows * rows),
         name="pair",
-    )(off, queries, out_grad, q_t, do_t, aux, kv)
+    )(off, queries, out_grad, aux, kv)
     returned = exchange(term)
     query_grad = pl.pallas_call(
         query_kernel,
         grid=(steps,),
         out_shape=jax.ShapeDtypeStruct(queries.shape, jnp.bfloat16),
-        in_specs=[kept, whole],
+        in_specs=[kept, keys_spec],
         out_specs=wide,
-        scratch_shapes=[
-            pltpu.VMEM((KVH * DH, rows), jnp.bfloat16),
-            pltpu.VMEM((rows, DH), jnp.bfloat16),
-        ],
+        scratch_shapes=[pltpu.VMEM((rows, DH), jnp.bfloat16)],
         compiler_params=big,
         cost_estimate=cost(matmul, wide_bytes + 2 * H * rows * rows),
         name="query",
-    )(ds, kv)
+    )(ds, keys)
+    returned, query_grad = lax.optimization_barrier((returned, query_grad))
     pooled = pl.pallas_call(
         pool_kernel,
         out_shape=low,

time: 115 us -> 112 us (0.974)
  blocking collectives: 41.2 us -> 19.4 us
  waiting for transfers between devices: 7.79 us -> 27.6 us
  Pallas kernels: 45.7 us -> 40.3 us
  starting transfers between devices: 16.1 us -> 20.6 us
    all_to_all x2 -> x1, blocking collectives: 41.2 us -> 19.4 us  [exchange(): return lax.all_to_all(x, AXES, split_axis=0, concat_axis=0, tiled=True)]
    all_to_all x2 -> x3, waiting for transfers between devices: 7.79 us -> 27.6 us  [exchange(): return lax.all_to_all(x, AXES, split_axis=0, concat_axis=0, tiled=True)]
    all_to_all x2 -> x3, starting transfers between devices: 16.1 us -> 20.6 us  [exchange(): return lax.all_to_all(x, AXES, split_axis=0, concat_axis=0, tiled=True)]
    pallas_call x1 -> x2, Pallas kernels: 10.1 us -> 6.69 us  [the longest x1 5.08 us: per_device(): pl.pallas_call(prep_kernel, grid=(steps,), out_shape=jax.ShapeDtypeStruct...]
    pallas_call x1, Pallas kernels: 10.5 us -> 8.5 us  [per_device(): pl.pallas_call(query_kernel, grid=(steps,), out_shape=jax.ShapeDtypeStruc...]
    unnamed x5 -> x9, local copies, waits for them, and re-layouts: 2.32 us -> 3.04 us
  transfers between devices with their start and end apart: 2 -> 3, of which waited for: 2 -> 3; matrix products, arithmetic and copies ran while one was open for 1% -> 1% of each run, Pallas kernels for 18% -> 14%
where the time goes in v3:
time: 112 us
  Pallas kernels  40.3 us (36%)
  waiting for transfers between devices  27.6 us (25%)
  starting transfers between devices  20.6 us (18%)
  blocking collectives  19.4 us (17%)
  local copies, waits for them, and re-layouts  3.04 us (3%)
    all_to_all x3, waiting for transfers between devices, exchange(): return lax.all_to_all(x, AXES, split_axis=0, concat_axis=0, tiled=True)  27.6 us
    all_to_all x3, starting transfers between devices, exchange(): return lax.all_to_all(x, AXES, split_axis=0, concat_axis=0, tiled=True)  20.6 us
    all_to_all x1, blocking collectives, exchange(): return lax.all_to_all(x, AXES, split_axis=0, concat_axis=0, tiled=True)  19.4 us
    pallas_call x1, Pallas kernels, per_device(): pl.pallas_call(pair_kernel, grid=(steps,), out_shape=(jax.ShapeDtypeStruc...  19.1 us
    pallas_call x1, Pallas kernels, per_device(): pl.pallas_call(query_kernel, grid=(steps,), out_shape=jax.ShapeDtypeStruc...  8.5 us
    pallas_call x1, Pallas kernels, per_device(): pl.pallas_call(prep_kernel, grid=(steps,), out_shape=jax.ShapeDtypeStruct...  5.08 us
    unnamed x9, local copies, waits for them, and re-layouts  3.04 us
  transfers between devices with their start and end apart: 3, of which 3 were waited for; matrix products, arithmetic and copies ran while one was open for 1% of the time, Pallas kernels for 14%

profile of v3, /device:TPU:1, one launch (start us, length us, event | category | flops | bytes accessed | tf_op | source)
XLA Modules:
  0.0 111.6 jit_solution(14683036698083852682)
XLA Ops:
  0.6 2.1 %spread.1 = bf16[128,4,640]{2,1,0:T(4,128)(2,1)} custom-call(bf16[640,256]{1,0:T(8,128)(2,1)} %k_hbm.1, bf16[640,256]{1,0:T(8,128)(2,1)} %v_hbm.1), custom_call_target="tpu_custom_call" | custom-call | tf_op jit(solution)/shard_map/spread/pallas_call | solution.py:224
  2.8 0.0 copy-start.3
  2.8 11.5 %all-to-all-start = ((bf16[128,4,640]{2,1,0:T(4,128)(2,1)}), bf16[128,4,640]{2,1,0:T(4,128)(2,1)S(1)}, u32[]{:S(2)}, u32[]{:S(2)}) async-start(bf16[128,4,640]{2,1,0:T(4,128)(2,1)} %spread.1), calls=%async_computation | async-start | bytes 1310720 | tf_op jit(solution)/shard_map/all_to_all | solution.py:195
  14.3 0.0 copy-start
  14.3 0.6 copy-done
  14.9 0.0 copy-start.1
  14.9 0.7 copy-done.1
  15.6 1.6 %table.1 = (s32[128]{0:T(128)S(1)}, s32[1]{0:T(128)}) custom-call(s32[1]{0:T(128)} %bitcast.own_ref, s32[128]{0:T(128)S(1)} %copy-done, s32[128]{0:T(128)S(1)} %copy-done.1), custom_call_target="tpu_custom_call" | custom-call | flops 1048576 | bytes 4096 | tf_op jit(solution)/shard_map/table/pallas_call | solution.py:238
  17.2 12.1 %all-to-all-done.in_ref = bf16[128,4,640]{2,1,0:T(4,128)(2,1)S(1)} async-done(((bf16[128,4,640]{2,1,0:T(4,128)(2,1)}), bf16[128,4,640]{2,1,0:T(4,128)(2,1)S(1)}, u32[]{:S(2)}, u32[]{:S(2)}) %all-to-all-start) | async-done | bytes 655392 | tf_op jit(solution)/shard_map/all_to_all | solution.py:195
  29.3 1.6 %select.1 = bf16[128,4,640]{2,1,0:T(4,128)(2,1)} custom-call(s32[128]{0:T(128)S(1)} %get-tuple-element.13.holder_ref, bf16[128,4,640]{2,1,0:T(4,128)(2,1)S(1)} %all-to-all-done.in_ref), custom_call_target="tpu_custom_call" | custom-call | tf_op jit(solution)/shard_map/select/pallas_call | solution.py:262
  30.9 4.6 %all-to-all-start.1 = ((bf16[128,4,640]{2,1,0:T(4,128)(2,1)}), bf16[128,4,640]{2,1,0:T(4,128)(2,1)S(1)}, u32[]{:S(2)}, u32[]{:S(2)}) async-start(bf16[128,4,640]{2,1,0:T(4,128)(2,1)} %select.1), calls=%async_computation.1 | async-start | bytes 1310720 | tf_op jit(solution)/shard_map/all_to_all | solution.py:195
  35.4 0.0 copy-done.3
  35.4 0.9 copy.11.norm_ref
  36.3 5.1 %prep.1.aux_ref = bf16[640,128]{1,0:T(8,128)(2,1)} custom-call(f32[640,16]{1,0:T(8,128)} %copy.11.norm_ref, bf16[640,2048]{1,0:T(8,128)(2,1)} %do_ref.3, bf16[640,2048]{1,0:T(8,128)(2,1)} %o_ref.1), custom_call_target="tpu_custom_call" | custom-call | flops 838860800 | bytes 5242880 | tf_op jit(solution)/shard_map/prep/pallas_call | solution.py:251
  41.4 9.0 %all-to-all-done.1.kv_ref = bf16[128,4,640]{2,1,0:T(4,128)(2,1)S(1)} async-done(((bf16[128,4,640]{2,1,0:T(4,128)(2,1)}), bf16[128,4,640]{2,1,0:T(4,128)(2,1)S(1)}, u32[]{:S(2)}, u32[]{:S(2)}) %all-to-all-start.1) | async-done | bytes 655392 | tf_op jit(solution)/shard_map/all_to_all | solution.py:195
  50.4 0.0 copy-start.2
  50.5 0.8 copy-done.2
  51.3 19.1 %pair.1 = (bf16[16,640,640]{2,1,0:T(8,128)(2,1)}, bf16[128,4,640]{2,1,0:T(4,128)(2,1)}, bf16[256,640]{1,0:T(8,128)(2,1)}) custom-call(s32[1]{0:T(128)} %get-tuple-element.12.off_ref, bf16[640,2048]{1,0:T(8,128)(2,1)} %q_ref.1, bf16[640,2048]{1,0:T(8,128)(2,1)} %do_ref.3, bf16[640,128]{1,0:T(8,128)(2,1)} %prep.1.aux_ref, bf16[128,4,640]{2,1,0:T(4,128)(2,1)} %copy-done.2), custom_call_target="tpu_custom_call" | custom-call | flops 6710886400 | bytes 23592960 | tf_op jit(solution)/shard_map/pair/pallas_call | solution.py:273
  70.4 4.6 %all-to-all-start.2 = ((bf16[128,4,640]{2,1,0:T(4,128)(2,1)}), bf16[128,4,640]{2,1,0:T(4,128)(2,1)S(1)}, u32[]{:S(2)}, u32[]{:S(2)}) async-start(bf16[128,4,640]{2,1,0:T(4,128)(2,1)} %get-tuple-element.14), calls=%async_computation.2 | async-start | bytes 1310720 | tf_op jit(solution)/shard_map/all_to_all | solution.py:195
  75.0 8.5 %query.1 = bf16[640,2048]{1,0:T(8,128)(2,1)} custom-call(bf16[16,640,640]{2,1,0:T(8,128)(2,1)} %get-tuple-element.15.ds_ref, bf16[256,640]{1,0:T(8,128)(2,1)} %get-tuple-element.16.keys_ref), custom_call_target="tpu_custom_call" | custom-call | flops 1677721600 | bytes 15728640 | tf_op jit(solution)/shard_map/query/pallas_call | solution.py:294
  83.5 6.5 %all-to-all-done.2.in_ref = bf16[128,4,640]{2,1,0:T(4,128)(2,1)S(1)} async-done(((bf16[128,4,640]{2,1,0:T(4,128)(2,1)}), bf16[128,4,640]{2,1,0:T(4,128)(2,1)S(1)}, u32[]{:S(2)}, u32[]{:S(2)}) %all-to-all-start.2) | async-done | bytes 655392 | tf_op jit(solution)/shard_map/all_to_all | solution.py:195
  90.0 1.2 %pool.1 = bf16[128,4,640]{2,1,0:T(4,128)(2,1)S(1)} custom-call(s32[128]{0:T(128)S(1)} %get-tuple-element.13.holder_ref, bf16[128,4,640]{2,1,0:T(4,128)(2,1)S(1)} %all-to-all-done.2.in_ref), custom_call_target="tpu_custom_call" | custom-call | tf_op jit(solution)/shard_map/pool/pallas_call | solution.py:306
  91.2 19.4 %all_to_all.20.in_ref = bf16[128,4,640]{2,1,0:T(4,128)(2,1)S(1)} all-to-all(bf16[128,4,640]{2,1,0:T(4,128)(2,1)S(1)} %pool.1), channel_id=1, replica_groups=mesh['grp'=16,'blk'=8] {'grp','blk'}, dimensions={0} | all-to-all | bytes 1310720 | tf_op jit(solution)/shard_map/all_to_all | solution.py:195
  110.6 1.0 finish.1
Async XLA Ops:
  2.8 32.7 %copy-start.3 = (f32[640,16]{0,1:T(8,128)S(1)}, f32[640,16]{0,1:T(8,128)}, u32[]{:S(2)}) copy-start(f32[640,16]{0,1:T(8,128)} %param.13) | copy-start | bytes 122884
  2.8 26.5 %all-to-all-start = ((bf16[128,4,640]{2,1,0:T(4,128)(2,1)}), bf16[128,4,640]{2,1,0:T(4,128)(2,1)S(1)}, u32[]{:S(2)}, u32[]{:S(2)}) async-start(bf16[128,4,640]{2,1,0:T(4,128)(2,1)} %spread.1), calls=%async_computation | async-start | bytes 1310720 | tf_op jit(solution)/shard_map/all_to_all | solution.py:195
  14.3 0.7 copy-start
  14.9 0.7 copy-start.1
  30.9 19.6 %all-to-all-start.1 = ((bf16[128,4,640]{2,1,0:T(4,128)(2,1)}), bf16[128,4,640]{2,1,0:T(4,128)(2,1)S(1)}, u32[]{:S(2)}, u32[]{:S(2)}) async-start(bf16[128,4,640]{2,1,0:T(4,128)(2,1)} %select.1), calls=%async_computation.1 | async-start | bytes 1310720 | tf_op jit(solution)/shard_map/all_to_all | solution.py:195
  50.4 0.8 copy-start.2
  70.4 19.6 %all-to-all-start.2 = ((bf16[128,4,640]{2,1,0:T(4,128)(2,1)}), bf16[128,4,640]{2,1,0:T(4,128)(2,1)S(1)}, u32[]{:S(2)}, u32[]{:S(2)}) async-start(bf16[128,4,640]{2,1,0:T(4,128)(2,1)} %get-tuple-element.14), calls=%async_computation.2 | async-start | bytes 1310720 | tf_op jit(solution)/shard_map/all_to_all | solution.py:195

commit v4 on v3

--- a/solution.py
+++ b/solution.py
@@ -121,7 +121,7 @@
 
 def pair_kernel(
     off_ref, q_ref, do_ref, aux_ref, kv_ref, ds_ref, term_ref, keys_ref,
-    flat_ref, bias_ref, dk_ref, dv_ref,
+    flat_ref, bias_ref, dk_ref, dv_ref, slot_ref, sems,
 ):
     step = pl.program_id(0)
     per_group = GROUP // STEP_HEADS
@@ -144,6 +144,18 @@
         dk_ref[...] = jnp.zeros_like(dk_ref)
         dv_ref[...] = jnp.zeros_like(dv_ref)
 
+    parity = step % 2
+
+    def write(sub, side):
+        return pltpu.make_async_copy(
+            slot_ref.at[side, sub], ds_ref.at[step * STEP_HEADS + sub], sems.at[side, sub]
+        )
+
+    @pl.when(step >= 2)
+    def _():
+        for sub in range(STEP_HEADS):
+            write(sub, parity).wait()
+
     k_t = flat_ref[pl.ds(pl.multiple_of(c * DH, DH), DH), :]
     v_t = flat_ref[pl.ds(pl.multiple_of((KVH + c) * DH, DH), DH), :]
     aux = aux_ref[...]
@@ -163,7 +175,8 @@
         dp = shifted(do_ref[:, cols], v_t, 1, head)
         p = jnp.exp2(s * (DH**-0.5 * LOG2E) + bias_ref[...])
         ds = (p * dp).astype(jnp.bfloat16)
-        ds_ref[sub] = ds
+        slot_ref[parity, sub] = ds
+        write(sub, parity).start()
         dv_ref[...] += jnp.dot(
             do_ref[:, cols].T, p.astype(jnp.bfloat16), preferred_element_type=jnp.float32
         )
@@ -175,6 +188,12 @@
         low_v = dv_ref[...].astype(term_ref.dtype)
         term_ref[pl.ds(c * pieces, pieces)] = low_k.reshape(pieces, depth, rows)
         term_ref[pl.ds((KVH + c) * pieces, pieces)] = low_v.reshape(pieces, depth, rows)
+
+    @pl.when(step == pl.num_programs(0) - 1)
+    def _():
+        for side in range(2):
+            for sub in range(STEP_HEADS):
+                write(sub, side).wait()
 
 
 def query_kernel(ds_ref, keys_ref, dq_ref, k_ref):
@@ -279,12 +298,14 @@
             jax.ShapeDtypeStruct((KVH * DH, rows), jnp.bfloat16),
         ),
         in_specs=[smem, wide, wide, aux_spec, whole],
-        out_specs=(kept, whole, keys_spec),
+        out_specs=(hbm, whole, keys_spec),
         scratch_shapes=[
             pltpu.VMEM((2 * KVH * DH, rows), jnp.bfloat16),
             pltpu.VMEM((rows, rows), jnp.float32),
             pltpu.VMEM((DH, rows), jnp.float32),
             pltpu.VMEM((DH, rows), jnp.float32),
+            pltpu.VMEM((2, STEP_HEADS, rows, rows), jnp.bfloat16),
+            pltpu.SemaphoreType.DMA((2, STEP_HEADS)),
         ],
         compiler_params=big,
         cost_estimate=cost(4 * matmul, 4 * wide_bytes + 2 * H * rows * rows),

time: 112 us -> 112 us (level)
  no operation moved by 1% of the time
where the time goes in v4:
time: 112 us; the launch traced here: 111 us
  Pallas kernels  39.8 us (36%)
  waiting for transfers between devices  27.6 us (25%)
  starting transfers between devices  20.6 us (18%)
  blocking collectives  19.4 us (17%)
  local copies, waits for them, and re-layouts  3.04 us (3%)
    all_to_all x3, waiting for transfers between devices, exchange(): return lax.all_to_all(x, AXES, split_axis=0, concat_axis=0, tiled=True)  27.6 us
    all_to_all x3, starting transfers between devices, exchange(): return lax.all_to_all(x, AXES, split_axis=0, concat_axis=0, tiled=True)  20.6 us
    all_to_all x1, blocking collectives, exchange(): return lax.all_to_all(x, AXES, split_axis=0, concat_axis=0, tiled=True)  19.4 us
    pallas_call x1, Pallas kernels, per_device(): pl.pallas_call(pair_kernel, grid=(steps,), out_shape=(jax.ShapeDtypeStruc...  18.7 us
    pallas_call x1, Pallas kernels, per_device(): pl.pallas_call(query_kernel, grid=(steps,), out_shape=jax.ShapeDtypeStruc...  8.5 us
    pallas_call x1, Pallas kernels, per_device(): pl.pallas_call(prep_kernel, grid=(steps,), out_shape=jax.ShapeDtypeStruct...  5.08 us
    unnamed x9, local copies, waits for them, and re-layouts  3.04 us
  transfers between devices with their start and end apart: 3, of which 3 were waited for; matrix products, arithmetic and copies ran while one was open for 1% of the time, Pallas kernels for 14%

profile of v4, /device:TPU:1, one launch (start us, length us, event | category | flops | bytes accessed | tf_op | source)
XLA Modules:
  0.0 111.2 jit_solution(4659042349286649944)
XLA Ops:
  0.6 2.1 %spread.1 = bf16[128,4,640]{2,1,0:T(4,128)(2,1)} custom-call(bf16[640,256]{1,0:T(8,128)(2,1)} %k_hbm.1, bf16[640,256]{1,0:T(8,128)(2,1)} %v_hbm.1), custom_call_target="tpu_custom_call" | custom-call | tf_op jit(solution)/shard_map/spread/pallas_call | solution.py:243
  2.8 0.0 copy-start.3
  2.8 11.5 %all-to-all-start = ((bf16[128,4,640]{2,1,0:T(4,128)(2,1)}), bf16[128,4,640]{2,1,0:T(4,128)(2,1)S(1)}, u32[]{:S(2)}, u32[]{:S(2)}) async-start(bf16[128,4,640]{2,1,0:T(4,128)(2,1)} %spread.1), calls=%async_computation | async-start | bytes 1310720 | tf_op jit(solution)/shard_map/all_to_all | solution.py:214
  14.3 0.0 copy-start
  14.3 0.6 copy-done
  14.9 0.0 copy-start.1
  14.9 0.7 copy-done.1
  15.6 1.6 %table.1 = (s32[128]{0:T(128)S(1)}, s32[1]{0:T(128)}) custom-call(s32[1]{0:T(128)} %bitcast.own_ref, s32[128]{0:T(128)S(1)} %copy-done, s32[128]{0:T(128)S(1)} %copy-done.1), custom_call_target="tpu_custom_call" | custom-call | flops 1048576 | bytes 4096 | tf_op jit(solution)/shard_map/table/pallas_call | solution.py:257
  17.2 12.1 %all-to-all-done.in_ref = bf16[128,4,640]{2,1,0:T(4,128)(2,1)S(1)} async-done(((bf16[128,4,640]{2,1,0:T(4,128)(2,1)}), bf16[128,4,640]{2,1,0:T(4,128)(2,1)S(1)}, u32[]{:S(2)}, u32[]{:S(2)}) %all-to-all-start) | async-done | bytes 655392 | tf_op jit(solution)/shard_map/all_to_all | solution.py:214
  29.3 1.6 %select.1 = bf16[128,4,640]{2,1,0:T(4,128)(2,1)} custom-call(s32[128]{0:T(128)S(1)} %get-tuple-element.13.holder_ref, bf16[128,4,640]{2,1,0:T(4,128)(2,1)S(1)} %all-to-all-done.in_ref), custom_call_target="tpu_custom_call" | custom-call | tf_op jit(solution)/shard_map/select/pallas_call | solution.py:281
  30.9 4.6 %all-to-all-start.1 = ((bf16[128,4,640]{2,1,0:T(4,128)(2,1)}), bf16[128,4,640]{2,1,0:T(4,128)(2,1)S(1)}, u32[]{:S(2)}, u32[]{:S(2)}) async-start(bf16[128,4,640]{2,1,0:T(4,128)(2,1)} %select.1), calls=%async_computation.1 | async-start | bytes 1310720 | tf_op jit(solution)/shard_map/all_to_all | solution.py:214
  35.4 0.0 copy-done.3
  35.4 0.9 copy.11.norm_ref
  36.3 5.1 %prep.1.aux_ref = bf16[640,128]{1,0:T(8,128)(2,1)} custom-call(f32[640,16]{1,0:T(8,128)} %copy.11.norm_ref, bf16[640,2048]{1,0:T(8,128)(2,1)} %do_ref.3, bf16[640,2048]{1,0:T(8,128)(2,1)} %o_ref.1), custom_call_target="tpu_custom_call" | custom-call | flops 838860800 | bytes 5242880 | tf_op jit(solution)/shard_map/prep/pallas_call | solution.py:270
  41.4 9.0 %all-to-all-done.1.kv_ref = bf16[128,4,640]{2,1,0:T(4,128)(2,1)S(1)} async-done(((bf16[128,4,640]{2,1,0:T(4,128)(2,1)}), bf16[128,4,640]{2,1,0:T(4,128)(2,1)S(1)}, u32[]{:S(2)}, u32[]{:S(2)}) %all-to-all-start.1) | async-done | bytes 655392 | tf_op jit(solution)/shard_map/all_to_all | solution.py:214
  50.4 0.0 copy-start.2
  50.5 0.8 copy-done.2
  51.3 18.7 %pair.1 = (bf16[16,640,640]{2,1,0:T(8,128)(2,1)}, bf16[128,4,640]{2,1,0:T(4,128)(2,1)}, bf16[256,640]{1,0:T(8,128)(2,1)}) custom-call(s32[1]{0:T(128)} %get-tuple-element.12.off_ref, bf16[640,2048]{1,0:T(8,128)(2,1)} %q_ref.1, bf16[640,2048]{1,0:T(8,128)(2,1)} %do_ref.3, bf16[640,128]{1,0:T(8,128)(2,1)} %prep.1.aux_ref, bf16[128,4,640]{2,1,0:T(4,128)(2,1)} %copy-done.2), custom_call_target="tpu_custom_call" | custom-call | flops 6710886400 | bytes 23592960 | tf_op jit(solution)/shard_map/pair/pallas_call | solution.py:292
  70.0 4.6 %all-to-all-start.2 = ((bf16[128,4,640]{2,1,0:T(4,128)(2,1)}), bf16[128,4,640]{2,1,0:T(4,128)(2,1)S(1)}, u32[]{:S(2)}, u32[]{:S(2)}) async-start(bf16[128,4,640]{2,1,0:T(4,128)(2,1)} %get-tuple-element.14), calls=%async_computation.2 | async-start | bytes 1310720 | tf_op jit(solution)/shard_map/all_to_all | solution.py:214
  74.6 8.5 %query.1 = bf16[640,2048]{1,0:T(8,128)(2,1)} custom-call(bf16[16,640,640]{2,1,0:T(8,128)(2,1)} %get-tuple-element.15.ds_ref, bf16[256,640]{1,0:T(8,128)(2,1)} %get-tuple-element.16.keys_ref), custom_call_target="tpu_custom_call" | custom-call | flops 1677721600 | bytes 15728640 | tf_op jit(solution)/shard_map/query/pallas_call | solution.py:315
  83.1 6.5 %all-to-all-done.2.in_ref = bf16[128,4,640]{2,1,0:T(4,128)(2,1)S(1)} async-done(((bf16[128,4,640]{2,1,0:T(4,128)(2,1)}), bf16[128,4,640]{2,1,0:T(4,128)(2,1)S(1)}, u32[]{:S(2)}, u32[]{:S(2)}) %all-to-all-start.2) | async-done | bytes 655392 | tf_op jit(solution)/shard_map/all_to_all | solution.py:214
  89.6 1.2 %pool.1 = bf16[128,4,640]{2,1,0:T(4,128)(2,1)S(1)} custom-call(s32[128]{0:T(128)S(1)} %get-tuple-element.13.holder_ref, bf16[128,4,640]{2,1,0:T(4,128)(2,1)S(1)} %all-to-all-done.2.in_ref), custom_call_target="tpu_custom_call" | custom-call | tf_op jit(solution)/shard_map/pool/pallas_call | solution.py:327
  90.9 19.4 %all_to_all.20.in_ref = bf16[128,4,640]{2,1,0:T(4,128)(2,1)S(1)} all-to-all(bf16[128,4,640]{2,1,0:T(4,128)(2,1)S(1)} %pool.1), channel_id=1, replica_groups=mesh['grp'=16,'blk'=8] {'grp','blk'}, dimensions={0} | all-to-all | bytes 1310720 | tf_op jit(solution)/shard_map/all_to_all | solution.py:214
  110.2 1.0 finish.1
Async XLA Ops:
  2.8 32.7 %copy-start.3 = (f32[640,16]{0,1:T(8,128)S(1)}, f32[640,16]{0,1:T(8,128)}, u32[]{:S(2)}) copy-start(f32[640,16]{0,1:T(8,128)} %param.13) | copy-start | bytes 122884
  2.8 26.5 %all-to-all-start = ((bf16[128,4,640]{2,1,0:T(4,128)(2,1)}), bf16[128,4,640]{2,1,0:T(4,128)(2,1)S(1)}, u32[]{:S(2)}, u32[]{:S(2)}) async-start(bf16[128,4,640]{2,1,0:T(4,128)(2,1)} %spread.1), calls=%async_computation | async-start | bytes 1310720 | tf_op jit(solution)/shard_map/all_to_all | solution.py:214
  14.3 0.7 copy-start
  14.9 0.7 copy-start.1
  30.9 19.6 %all-to-all-start.1 = ((bf16[128,4,640]{2,1,0:T(4,128)(2,1)}), bf16[128,4,640]{2,1,0:T(4,128)(2,1)S(1)}, u32[]{:S(2)}, u32[]{:S(2)}) async-start(bf16[128,4,640]{2,1,0:T(4,128)(2,1)} %select.1), calls=%async_computation.1 | async-start | bytes 1310720 | tf_op jit(solution)/shard_map/all_to_all | solution.py:214
  50.4 0.8 copy-start.2
  70.0 19.6 %all-to-all-start.2 = ((bf16[128,4,640]{2,1,0:T(4,128)(2,1)}), bf16[128,4,640]{2,1,0:T(4,128)(2,1)S(1)}, u32[]{:S(2)}, u32[]{:S(2)}) async-start(bf16[128,4,640]{2,1,0:T(4,128)(2,1)} %get-tuple-element.14), calls=%async_computation.2 | async-start | bytes 1310720 | tf_op jit(solution)/shard_map/all_to_all | solution.py:214
